TPU v7x, 32 devices: a whole 2x2x4 slice. The times are simulated.
32 devices in a mesh: dp: 4 (over z), seq: 4 (over y, core), tensor: 2 (over x).
Axes of the slice: x: 2, y: 2, z: 4, core: 2. Of those that a mesh axis runs over, the one named last changes fastest.
Arguments:
- tokens: bfloat16 [4, 512, 2048], P('dp', 'seq'), may hold values from -6 to 6
- positions: int32 [4, 512], P('dp', 'seq'), may hold values from 0 to 1533, as said below
- gain_attn: bfloat16 [1, 2048], P(None, ('dp', 'seq')), may hold values from 0.5 to 1.5
- gain_ffn: bfloat16 [1, 2048], P(None, ('dp', 'seq')), may hold values from 0.5 to 1.5
- w_query: bfloat16 [1, 2048, 2048], P(None, ('dp', 'seq'), 'tensor'), may hold values from -1 to 1
- w_key: bfloat16 [1, 2048, 512], P(None, ('dp', 'seq'), 'tensor'), may hold values from -1 to 1
- w_value: bfloat16 [1, 2048, 512], P(None, ('dp', 'seq'), 'tensor'), may hold values from -0.125 to 0.125
- w_out: bfloat16 [1, 2048, 2048], P(None, ('dp', 'seq'), 'tensor'), may hold values from -0.75 to 0.75
- w_gate: bfloat16 [1, 2048, 8192], P(None, ('dp', 'seq'), 'tensor'), may hold values from -0.125 to 0.125
- w_up: bfloat16 [1, 2048, 8192], P(None, ('dp', 'seq'), 'tensor'), may hold values from -0.125 to 0.125
- w_down: bfloat16 [1, 2048, 8192], P(None, ('dp', 'seq'), 'tensor'), may hold values from -0.0625 to 0.0625
- cotangent: bfloat16 [4, 512, 2048], P('dp', 'seq'), may hold values from -6 to 6
Outputs:
- activations: bfloat16 [4, 512, 2048], P('dp', 'seq')
- input_grad: float32 [4, 512, 2048], P('dp', 'seq')
- grad_gain_attn: float32 [1, 2048], P(None, ('dp', 'seq'))
- grad_gain_ffn: float32 [1, 2048], P(None, ('dp', 'seq'))
- grad_query: float32 [1, 2048, 2048], P(None, ('dp', 'seq'), 'tensor')
- grad_key: float32 [1, 2048, 512], P(None, ('dp', 'seq'), 'tensor')
- grad_value: float32 [1, 2048, 512], P(None, ('dp', 'seq'), 'tensor')
- grad_out: float32 [1, 2048, 2048], P(None, ('dp', 'seq'), 'tensor')
- grad_gate: float32 [1, 2048, 8192], P(None, ('dp', 'seq'), 'tensor')
- grad_up: float32 [1, 2048, 8192], P(None, ('dp', 'seq'), 'tensor')
- grad_down: float32 [1, 2048, 8192], P(None, ('dp', 'seq'), 'tensor')
Inputs may be any that keep to these rules, and one draw needn't show every extreme that they name: In each sequence positions start at 0 and rise by 1 to 3 from one token to the next; the first sequence rises by 3 throughout.
All inputs are finite; a program needn't handle non-finite values.
Results may differ from a plain program's by a relative error of at most 0.018.
The roundings to bfloat16 on the way count: a program that leaves them out, or rounds other values in their place, can miss the bound.
Values may be sent and summed in bfloat16 or wider, within the bound.
A program may use at most 320 MiB of HBM per device.

v0:
```python
import jax
import jax.numpy as jnp
from jax import lax
from jax.sharding import PartitionSpec as P

HD = 64


epsilon = 1e-05
rope_base = 500000.0


def norm_forward(stream, gain):
    inverse = lax.rsqrt(jnp.mean(stream * stream, axis=-1, keepdims=True) + epsilon)
    return ((stream * inverse * gain.astype(jnp.float32)).astype(jnp.bfloat16), inverse)


def norm_backward(stream, inverse, gain, normed_grad):
    unit_rms = stream * inverse
    gain_grad = jnp.sum(normed_grad * unit_rms, axis=0)
    scaled = normed_grad * gain.astype(jnp.float32)
    return (
        inverse * (scaled - unit_rms * jnp.mean(scaled * unit_rms, axis=-1, keepdims=True)),
        gain_grad,
    )


def rope_tables(position, head_dim):
    half_dim = head_dim // 2
    frequency = rope_base ** (-jnp.arange(half_dim, dtype=jnp.float32) / half_dim)
    angles = position.astype(jnp.float32)[:, None] * frequency[None, :]
    return (jnp.cos(angles)[:, None, :], jnp.sin(angles)[:, None, :])


def rotate(values, cosine, sine_table, direction):
    half_dim = values.shape[-1] // 2
    first_half = values[..., :half_dim]
    second_half = values[..., half_dim:]
    return jnp.concatenate(
        [
            first_half * cosine - direction * second_half * sine_table,
            second_half * cosine + direction * first_half * sine_table,
        ],
        axis=-1,
    )


def contract_last(left_matrix, right_matrix):
    return lax.dot_general(
        left_matrix, right_matrix, (((1,), (1,)), ((), ())), preferred_element_type=jnp.float32
    )


def contract_rows(left_matrix, right_matrix):
    return lax.dot_general(
        left_matrix, right_matrix, (((0,), (0,)), ((), ())), preferred_element_type=jnp.float32
    )


def tensor_sum(partial_sum):
    return lax.psum(partial_sum, "tensor")


def head_scores(query_head, key_head, q_index):
    score_scale = query_head.shape[-1] ** (-0.5)
    raw_scores = (
        jnp.einsum("qgd,kd->gqk", query_head, key_head, preferred_element_type=jnp.float32)
        * score_scale
    )
    allowed = q_index[:, None] >= jnp.arange(key_head.shape[0], dtype=jnp.int32)[None, :]
    return jnp.where(allowed[None], raw_scores, -1e30)


def attend(queries, keys_all, values_all, q_index):

    def one_head(operands):
        query_head, key_head, value_head = operands
        scores = head_scores(query_head, key_head, q_index)
        row_peak = jnp.max(scores, axis=-1, keepdims=True)
        exps = jnp.exp(scores - row_peak)
        totals = jnp.sum(exps, axis=-1, keepdims=True)
        probability = (exps / totals).astype(jnp.bfloat16)
        attended = jnp.einsum(
            "gqk,kd->qgd", probability, value_head, preferred_element_type=jnp.float32
        )
        return (attended.astype(jnp.bfloat16), (row_peak + jnp.log(totals))[..., 0])

    attended, logsum = lax.map(
        one_head,
        (jnp.moveaxis(queries, 1, 0), jnp.moveaxis(keys_all, 1, 0), jnp.moveaxis(values_all, 1, 0)),
    )
    return (jnp.moveaxis(attended, 0, 1), logsum)


def attend_back(queries, keys_all, values_all, attended, attended_grad, logsum, q_index):

    def one_head(operands):
        query_head, key_head, value_head, mixed_head, grad_head, logsum_head = operands
        score_scale = query_head.shape[-1] ** (-0.5)
        probability = jnp.exp(head_scores(query_head, key_head, q_index) - logsum_head[..., None])
        value_grad = jnp.einsum(
            "gqk,qgd->kd",
            probability.astype(jnp.bfloat16),
            grad_head,
            preferred_element_type=jnp.float32,
        )
        prob_grad = jnp.einsum(
            "qgd,kd->gqk", grad_head, value_head, preferred_element_type=jnp.float32
        )
        row_dots = jnp.sum(grad_head.astype(jnp.float32) * mixed_head.astype(jnp.float32), axis=-1)
        score_grad = (probability * (prob_grad - row_dots.T[:, :, None]) * score_scale).astype(
            jnp.bfloat16
        )
        query_grad = jnp.einsum(
            "gqk,kd->qgd", score_grad, key_head, preferred_element_type=jnp.float32
        )
        key_grad = jnp.einsum(
            "gqk,qgd->kd", score_grad, query_head, preferred_element_type=jnp.float32
        )
        return (query_grad, key_grad, value_grad)

    query_grad, key_grad, value_grad = lax.map(
        one_head,
        (
            jnp.moveaxis(queries, 1, 0),
            jnp.moveaxis(keys_all, 1, 0),
            jnp.moveaxis(values_all, 1, 0),
            jnp.moveaxis(attended, 1, 0),
            jnp.moveaxis(attended_grad, 1, 0),
            logsum,
        ),
    )
    return (
        jnp.moveaxis(query_grad, 0, 1),
        jnp.moveaxis(key_grad, 0, 1),
        jnp.moveaxis(value_grad, 0, 1),
    )


def layer_forward(stream, cosine, sine_table, q_index, weights):
    gain_one, gain_two, w_q, w_k, w_v, w_o, w_g, w_u, w_d = weights
    row_count = stream.shape[0]
    head_count = w_q.shape[1] // HD
    groups = w_k.shape[1] // HD
    normed_one, inverse_one = norm_forward(stream, gain_one)
    queries = rotate(
        jnp.dot(normed_one, w_q, preferred_element_type=jnp.float32).reshape(
            row_count, head_count, HD
        ),
        cosine,
        sine_table,
        1.0,
    ).astype(jnp.bfloat16)
    keys_own = rotate(
        jnp.dot(normed_one, w_k, preferred_element_type=jnp.float32).reshape(row_count, groups, HD),
        cosine,
        sine_table,
        1.0,
    ).astype(jnp.bfloat16)
    values_own = jnp.dot(normed_one, w_v, preferred_element_type=jnp.float32).astype(jnp.bfloat16)
    keys_all, values_all = (
        lax.all_gather(keys_own.reshape(row_count, groups * HD), "seq", axis=0, tiled=True),
        lax.all_gather(values_own, "seq", axis=0, tiled=True),
    )
    length = keys_all.shape[0]
    keys_all = keys_all.reshape(length, groups, HD)
    values_all = values_all.reshape(length, groups, HD)
    attended, logsum = attend(
        queries.reshape(row_count, groups, head_count // groups, HD), keys_all, values_all, q_index
    )
    attended = attended.reshape(row_count, head_count * HD)
    after_attn = stream + tensor_sum(contract_last(attended, w_o))
    normed_two, inverse_two = norm_forward(after_attn, gain_two)
    gate_pre = jnp.dot(normed_two, w_g, preferred_element_type=jnp.float32)
    up_proj = jnp.dot(normed_two, w_u, preferred_element_type=jnp.float32)
    hidden = (jax.nn.silu(gate_pre) * up_proj).astype(jnp.bfloat16)
    output = after_attn + tensor_sum(contract_last(hidden, w_d))
    kept_state = (
        stream,
        inverse_one,
        normed_one,
        queries,
        keys_all,
        values_all,
        attended,
        logsum,
        after_attn,
        inverse_two,
        normed_two,
        gate_pre,
        up_proj,
        hidden,
    )
    return (output, kept_state)


def layer_backward(out_grad, kept_state, cosine, sine_table, q_index, weights):
    gain_one, gain_two, w_q, w_k, w_v, w_o, w_g, w_u, w_d = weights
    (
        stream,
        inverse_one,
        normed_one,
        queries,
        keys_all,
        values_all,
        attended,
        logsum,
        after_attn,
        inverse_two,
        normed_two,
        gate_pre,
        up_proj,
        hidden,
    ) = kept_state
    row_count = stream.shape[0]
    head_count = w_q.shape[1] // HD
    groups = w_k.shape[1] // HD
    length = keys_all.shape[0]
    low_grad = out_grad.astype(jnp.bfloat16)
    down_grad = contract_rows(low_grad, hidden)
    hidden_grad = jnp.dot(low_grad, w_d, preferred_element_type=jnp.float32)
    sigmoid_gate = jax.nn.sigmoid(gate_pre)
    gate_grad = (
        hidden_grad * up_proj * sigmoid_gate * (1.0 + gate_pre * (1.0 - sigmoid_gate))
    ).astype(jnp.bfloat16)
    up_grad = (hidden_grad * gate_pre * sigmoid_gate).astype(jnp.bfloat16)
    wgate_grad = contract_rows(normed_two, gate_grad)
    wup_grad = contract_rows(normed_two, up_grad)
    normed_two_grad = tensor_sum(contract_last(gate_grad, w_g) + contract_last(up_grad, w_u))
    resid_part, gain_two_grad = norm_backward(after_attn, inverse_two, gain_two, normed_two_grad)
    resid_grad = out_grad + resid_part
    resid_low = resid_grad.astype(jnp.bfloat16)
    wout_grad = contract_rows(resid_low, attended)
    attended_grad = jnp.dot(resid_low, w_o, preferred_element_type=jnp.float32).astype(jnp.bfloat16)
    group_shape = (row_count, groups, head_count // groups, HD)
    query_grad, key_grad, value_grad = attend_back(
        queries.reshape(group_shape),
        keys_all,
        values_all,
        attended.reshape(group_shape),
        attended_grad.reshape(group_shape),
        logsum,
        q_index,
    )
    key_grad, value_grad = (
        lax.psum_scatter(
            key_grad.reshape(length, groups * HD).astype(jnp.bfloat16),
            "seq",
            scatter_dimension=0,
            tiled=True,
        ).astype(jnp.float32),
        lax.psum_scatter(
            value_grad.reshape(length, groups * HD).astype(jnp.bfloat16),
            "seq",
            scatter_dimension=0,
            tiled=True,
        ).astype(jnp.float32),
    )
    query_grad = (
        rotate(query_grad.reshape(row_count, head_count, HD), cosine, sine_table, -1.0)
        .astype(jnp.bfloat16)
        .reshape(row_count, head_count * HD)
    )
    key_grad = (
        rotate(key_grad.reshape(row_count, groups, HD), cosine, sine_table, -1.0)
        .astype(jnp.bfloat16)
        .reshape(row_count, groups * HD)
    )
    value_grad = value_grad.astype(jnp.bfloat16)
    wq_grad = contract_rows(normed_one, query_grad)
    wk_grad = contract_rows(normed_one, key_grad)
    wv_grad = contract_rows(normed_one, value_grad)
    normed_one_grad = tensor_sum(
        contract_last(query_grad, w_q)
        + contract_last(key_grad, w_k)
        + contract_last(value_grad, w_v)
    )
    input_part, gain_one_grad = norm_backward(stream, inverse_one, gain_one, normed_one_grad)
    return (
        resid_grad + input_part,
        (
            gain_one_grad,
            gain_two_grad,
            wq_grad,
            wk_grad,
            wv_grad,
            wout_grad,
            wgate_grad,
            wup_grad,
            down_grad,
        ),
    )


def shards(
    tokens,
    positions,
    gain_attn,
    gain_ffn,
    w_query,
    w_key,
    w_value,
    w_out,
    w_gate,
    w_up,
    w_down,
    cotangent,
):
    piece = tokens.shape[1]
    layer_total = w_query.shape[0]
    stream = tokens[0].astype(jnp.float32)
    cosine, sine_table = rope_tables(positions[0], HD)
    q_index = lax.axis_index("seq") * piece + jnp.arange(piece, dtype=jnp.int32)

    def fetch(layer_at):
        return (
            lax.all_gather(gain_attn[layer_at], ("dp", "seq"), axis=0, tiled=True),
            lax.all_gather(gain_ffn[layer_at], ("dp", "seq"), axis=0, tiled=True),
            lax.all_gather(w_query[layer_at], ("dp", "seq"), axis=0, tiled=True),
            lax.all_gather(w_key[layer_at], ("dp", "seq"), axis=0, tiled=True),
            lax.all_gather(w_value[layer_at], ("dp", "seq"), axis=0, tiled=True),
            lax.all_gather(w_out[layer_at], ("dp", "seq"), axis=0, tiled=True),
            lax.all_gather(w_gate[layer_at], ("dp", "seq"), axis=0, tiled=True),
            lax.all_gather(w_up[layer_at], ("dp", "seq"), axis=0, tiled=True),
            lax.all_gather(w_down[layer_at], ("dp", "seq"), axis=0, tiled=True),
        )

    weights = None
    layer_at = 0
    weights = fetch(layer_at)
    stream, kept_state = layer_forward(stream, cosine, sine_table, q_index, weights)
    states = [kept_state]
    carried = cotangent[0].astype(jnp.float32)
    layer_grads = [None] * layer_total
    for layer_at in reversed(range(layer_total)):
        weights = fetch(layer_at)
        carried, terms = layer_backward(
            carried, states[layer_at], cosine, sine_table, q_index, weights
        )
        layer_grads[layer_at] = (
            lax.psum_scatter(terms[0], ("dp", "seq"), scatter_dimension=0, tiled=True),
            lax.psum_scatter(terms[1], ("dp", "seq"), scatter_dimension=0, tiled=True),
            lax.psum_scatter(terms[2], ("dp", "seq"), scatter_dimension=0, tiled=True),
            lax.psum_scatter(terms[3], ("dp", "seq"), scatter_dimension=0, tiled=True),
            lax.psum_scatter(terms[4], ("dp", "seq"), scatter_dimension=0, tiled=True),
            lax.psum_scatter(terms[5], ("dp", "seq"), scatter_dimension=0, tiled=True),
            lax.psum_scatter(terms[6], ("dp", "seq"), scatter_dimension=0, tiled=True),
            lax.psum_scatter(terms[7], ("dp", "seq"), scatter_dimension=0, tiled=True),
            lax.psum_scatter(terms[8], ("dp", "seq"), scatter_dimension=0, tiled=True),
        )
    stacked = tuple((jnp.stack([layer_grads[0][member]]) for member in range(9)))
    return (
        stream.astype(jnp.bfloat16)[None],
        carried[None],
        stacked[0],
        stacked[1],
        stacked[2],
        stacked[3],
        stacked[4],
        stacked[5],
        stacked[6],
        stacked[7],
        stacked[8],
    )


def solution(mesh):
    in_specs = (
        P("dp", "seq", None),
        P("dp", "seq"),
        P(None, ("dp", "seq")),
        P(None, ("dp", "seq")),
        P(None, ("dp", "seq"), "tensor"),
        P(None, ("dp", "seq"), "tensor"),
        P(None, ("dp", "seq"), "tensor"),
        P(None, ("dp", "seq"), "tensor"),
        P(None, ("dp", "seq"), "tensor"),
        P(None, ("dp", "seq"), "tensor"),
        P(None, ("dp", "seq"), "tensor"),
        P("dp", "seq", None),
    )
    out_specs = (
        P("dp", "seq", None),
        P("dp", "seq", None),
        P(None, ("dp", "seq")),
        P(None, ("dp", "seq")),
        P(None, ("dp", "seq"), "tensor"),
        P(None, ("dp", "seq"), "tensor"),
        P(None, ("dp", "seq"), "tensor"),
        P(None, ("dp", "seq"), "tensor"),
        P(None, ("dp", "seq"), "tensor"),
        P(None, ("dp", "seq"), "tensor"),
        P(None, ("dp", "seq"), "tensor"),
    )
    return jax.shard_map(shards, mesh=mesh, in_specs=in_specs, out_specs=out_specs, check_vma=False)
```

profile of v0, /device:TPU:9, one launch (start us, length us, event | category | flops | bytes accessed | tf_op | source)
XLA Modules:
  0.0 2198.8 jit_solution(7090537279936444482)
XLA Ops:
  10.1 19.5 all-gather
  31.7 16.9 all-gather.17.cloned.1.call-done
  56.4 31.2 %all-gather.19.cloned.1.call-done = bf16[1,2048,256]{2,1,0:T(8,128)(2,1)} async-done(((bf16[1,128,256]{2,1,0:T(8,128)(2,1)}), bf16[1,2048,256]{2,1,0:T(8,128)(2,1)}) %all-gather.19.cloned.1.call-update) | async-done | bytes 1048592 | tf_op jit(solution)/shard_map/all_gather | solution.py:320
  89.7 5.9 all_gather.46
  95.6 44.6 %all-gather.21.cloned.1.call-done = bf16[1,2048,1024]{2,1,0:T(8,128)(2,1)} async-done(((bf16[1,128,1024]{2,1,0:T(8,128)(2,1)}), bf16[1,2048,1024]{2,1,0:T(8,128)(2,1)}) %all-gather.21.cloned.1.call-update) | async-done | bytes 4194320 | tf_op jit(solution)/shard_map/all_gather | solution.py:319
  140.3 6.5 copy.47
  154.3 36.9 %all-gather.23.cloned.1.call-done = bf16[1,2048,1024]{2,1,0:T(8,128)(2,1)} async-done(((bf16[1,128,1024]{2,1,0:T(8,128)(2,1)}), bf16[1,2048,1024]{2,1,0:T(8,128)(2,1)}) %all-gather.23.cloned.1.call-update) | async-done | bytes 4194320 | tf_op jit(solution)/shard_map/all_gather | solution.py:322
  198.1 16.4 all-gather.5
  214.6 19.5 all-reduce.8.cloned.1.call-done
  235.8 125.7 %all-gather.29.cloned.1.call-done = bf16[1,2048,4096]{2,1,0:T(8,128)(2,1)} async-done(((bf16[1,128,4096]{2,1,0:T(8,128)(2,1)}), bf16[1,2048,4096]{2,1,0:T(8,128)(2,1)}) %all-gather.29.cloned.1.call-update) | async-done | bytes 16777232 | tf_op jit(solution)/shard_map/all_gather | solution.py:325
  361.5 9.4 fusion.50
  370.9 117.4 %all-gather.27.cloned.1.call-done = bf16[1,2048,4096]{2,1,0:T(8,128)(2,1)} async-done(((bf16[1,128,4096]{2,1,0:T(8,128)(2,1)}), bf16[1,2048,4096]{2,1,0:T(8,128)(2,1)}) %all-gather.27.cloned.1.call-update) | async-done | bytes 16777232 | tf_op jit(solution)/shard_map/all_gather | solution.py:324
  488.3 9.4 fusion.56
  497.7 117.4 %all-gather.25.cloned.1.call-done = bf16[1,2048,4096]{2,1,0:T(8,128)(2,1)} async-done(((bf16[1,128,4096]{2,1,0:T(8,128)(2,1)}), bf16[1,2048,4096]{2,1,0:T(8,128)(2,1)}) %all-gather.25.cloned.1.call-update) | async-done | bytes 16777232 | tf_op jit(solution)/shard_map/all_gather | solution.py:323
  615.1 11.8 multiply_convert_fusion.1
  626.9 12.9 fusion.54
  639.9 12.9 fusion.74
  652.9 39.5 %all-reduce.10.cloned.1.call-done = f32[128,2048]{1,0:T(8,128)} async-done(((f32[128,2048]{1,0:T(8,128)}), f32[128,2048]{1,0:T(8,128)}) %all-reduce.10.cloned.1.call-update) | async-done | bytes 1048592 | tf_op jit(solution)/shard_map/psum | solution.py:61
  698.4 31.5 %while.29 = (s32[]{:T(128)}, f32[4,128,4,64]{1,3,2,0:T(8,128)}, bf16[4,512,64]{1,2,0:T(8,128)(2,1)}, bf16[4,512,64]{1,2,0:T(8,128)(2,1)}, bf16[4,512,64]{1,2,0:T...) while((s32[]{:T(128)}, f32[4,128,4,64]{1,3,2,0:T(8,128)}, ...), condition=%wide.region_12.13_spmd.clone, body=%wide.region_10.12_spmd.clone.sunk | while | flops 170065536 | bytes 7946433 | solution.py:122
  731.8 12.8 fusion.52
  752.9 22.1 %reduce-scatter.30.cloned.1.call-done = bf16[128,256]{1,0:T(8,128)(2,1)} async-done(((bf16[512,256]{1,0:T(8,128)(2,1)}), bf16[128,256]{1,0:T(8,128)(2,1)}) %reduce-scatter.30.cloned.1.call-update) | async-done | bytes 65552
  781.2 17.5 convolution_bitcast_fusion.4
  814.1 15.3 fusion.125
  829.7 14.4 fusion.126
  847.6 48.3 %all-reduce.2 = (f32[2048]{0:T(1024)S(1)}, f32[2048]{0:T(1024)S(1)}) all-reduce(f32[2048]{0:T(1024)S(1)} %get-tuple-element.190, f32[2048]{0:T(1024)S(1)} %get-tuple-element.188), channel_id=13, replica_groups=mesh['dp'=4,'seq'=4,'tensor'=2] {'dp','seq'}, use_global_device_ids=true, to_apply=%region_18.19.clone | all-reduce | flops 4096 | bytes 32768
  899.9 278.3 %reduce-scatter.26.cloned.1.call-done = f32[128,4096]{0,1:T(8,128)} async-done(((f32[2048,4096]{0,1:T(8,128)}), f32[128,4096]{0,1:T(8,128)}) %reduce-scatter.26.cloned.1.call-update) | async-done | bytes 2097168 | tf_op jit(solution)/shard_map/reduce_scatter | solution.py:349
  1181.1 60.9 %reduce-scatter.16.cloned.1.call-done = f32[128,256]{1,0:T(8,128)} async-done(((f32[2048,256]{1,0:T(8,128)}), f32[128,256]{1,0:T(8,128)}) %reduce-scatter.16.cloned.1.call-update) | async-done | bytes 131088 | tf_op jit(solution)/shard_map/reduce_scatter | solution.py:344
  1242.0 64.9 %reduce-scatter.18.cloned.1.call-done = f32[128,256]{1,0:T(8,128)} async-done(((f32[2048,256]{1,0:T(8,128)}), f32[128,256]{1,0:T(8,128)}) %reduce-scatter.18.cloned.1.call-update) | async-done | bytes 131088 | tf_op jit(solution)/shard_map/reduce_scatter | solution.py:345
  1306.9 109.0 %reduce-scatter.14.cloned.1.call-done = f32[128,1024]{1,0:T(8,128)} async-done(((f32[2048,1024]{1,0:T(8,128)}), f32[128,1024]{1,0:T(8,128)}) %reduce-scatter.14.cloned.1.call-update) | async-done | bytes 524304 | tf_op jit(solution)/shard_map/reduce_scatter | solution.py:343
  1415.9 107.6 %reduce-scatter.20.cloned.1.call-done = f32[128,1024]{1,0:T(8,128)} async-done(((f32[2048,1024]{1,0:T(8,128)}), f32[128,1024]{1,0:T(8,128)}) %reduce-scatter.20.cloned.1.call-update) | async-done | bytes 524304 | tf_op jit(solution)/shard_map/reduce_scatter | solution.py:346
  1523.5 334.1 %reduce-scatter.22.cloned.1.call-done = f32[128,4096]{1,0:T(8,128)} async-done(((f32[2048,4096]{1,0:T(8,128)}), f32[128,4096]{1,0:T(8,128)}) %reduce-scatter.22.cloned.1.call-update) | async-done | bytes 2097168 | tf_op jit(solution)/shard_map/reduce_scatter | solution.py:347
  1857.6 334.5 %reduce-scatter.24.cloned.1.call-done = f32[128,4096]{1,0:T(8,128)} async-done(((f32[2048,4096]{1,0:T(8,128)}), f32[128,4096]{1,0:T(8,128)}) %reduce-scatter.24.cloned.1.call-update) | async-done | bytes 2097168 | tf_op jit(solution)/shard_map/reduce_scatter | solution.py:348
  (201 shorter events, 113.1 us)
Async XLA Ops:
  7.2 82.0 %copy-start = (bf16[1,128,2048]{2,1,0:T(8,128)(2,1)S(1)}, bf16[1,128,2048]{2,1,0:T(8,128)(2,1)}, u32[]{:S(2)}) copy-start(bf16[1,128,2048]{2,1,0:T(8,128)(2,1)} %param.16) | copy-start | bytes 1572868
  7.2 41.4 %all-gather.17.cloned.1.call-start = ((), (), s32[]{:S(2)}) async-start(), calls=%async_computation.18 | async-start | bytes 1114112 | tf_op jit(solution)/shard_map/all_gather | solution.py:321
  7.9 79.7 %all-gather.19.cloned.1.call-start = ((), (), s32[]{:S(2)}) async-start(), calls=%async_computation.19 | async-start | bytes 1114112 | tf_op jit(solution)/shard_map/all_gather | solution.py:320
  8.7 131.6 %all-gather.21.cloned.1.call-start = ((), (), s32[]{:S(2)}) async-start(), calls=%async_computation.20 | async-start | bytes 4456448 | tf_op jit(solution)/shard_map/all_gather | solution.py:319
  9.4 181.8 %all-gather.23.cloned.1.call-start = ((), (), s32[]{:S(2)}) async-start(), calls=%async_computation.21 | async-start | bytes 4456448 | tf_op jit(solution)/shard_map/all_gather | solution.py:322
  10.0 224.1 %all-reduce.8.cloned.1.call-start = ((), (), s32[]{:S(2)}) async-start(), calls=%async_computation.9 | async-start | bytes 2097152 | tf_op jit(solution)/shard_map/psum | solution.py:61
  30.9 115.9 %copy-start.14 = (f32[128]{0:T(128)}, f32[128]{0:T(128)S(1)}, u32[]{:S(2)}) copy-start(f32[128]{0:T(128)S(1)} %add_rsqrt_fusion.1) | copy-start | bytes 1540
  154.3 41.7 %copy-start.5 = (bf16[4,128,4,64]{1,3,2,0:T(8,128)(2,1)}, bf16[4,128,4,64]{1,3,2,0:T(8,128)(2,1)S(1)}, u32[]{:S(2)}) copy-start(bf16[4,128,4,64]{1,3,2,0:T(8,128)(2,1)S(1)} %get-tuple-element.401) | copy-start | bytes 786436
  154.3 41.7 %copy-start.7 = (bf16[4,512,64]{1,2,0:T(8,128)(2,1)}, bf16[4,512,64]{1,2,0:T(8,128)(2,1)S(1)}, u32[]{:S(2)}) copy-start(bf16[4,512,64]{1,2,0:T(8,128)(2,1)S(1)} %get-tuple-element.482) | copy-start | bytes 786436
  154.3 43.0 %copy-start.8 = (bf16[4,512,64]{1,2,0:T(8,128)(2,1)}, bf16[4,512,64]{1,2,0:T(8,128)(2,1)S(1)}, u32[]{:S(2)}) copy-start(bf16[4,512,64]{1,2,0:T(8,128)(2,1)S(1)} %get-tuple-element.483) | copy-start | bytes 786436
  154.3 43.0 %copy-start.9 = (bf16[4,128,4,64]{1,3,2,0:T(8,128)(2,1)}, bf16[4,128,4,64]{1,3,2,0:T(8,128)(2,1)S(1)}, u32[]{:S(2)}) copy-start(bf16[4,128,4,64]{1,3,2,0:T(8,128)(2,1)S(1)} %get-tuple-element.484) | copy-start | bytes 786436
  195.9 165.5 %copy-start.3 = (bf16[1,128,2048]{2,1,0:T(8,128)(2,1)S(1)}, bf16[1,128,2048]{2,1,0:T(8,128)(2,1)}, u32[]{:S(2)}) copy-start(bf16[1,128,2048]{2,1,0:T(8,128)(2,1)} %param.27) | copy-start | bytes 1572868
  196.0 165.5 %all-gather.29.cloned.1.call-start = ((), (), s32[]{:S(2)}) async-start(), calls=%async_computation.24 | async-start | bytes 17825792 | tf_op jit(solution)/shard_map/all_gather | solution.py:325
  196.6 291.7 %all-gather.27.cloned.1.call-start = ((), (), s32[]{:S(2)}) async-start(), calls=%async_computation.23 | async-start | bytes 17825792 | tf_op jit(solution)/shard_map/all_gather | solution.py:324
  197.3 417.7 %all-gather.25.cloned.1.call-start = ((), (), s32[]{:S(2)}) async-start(), calls=%async_computation.22 | async-start | bytes 17825792 | tf_op jit(solution)/shard_map/all_gather | solution.py:323
  198.1 494.3 %all-reduce.10.cloned.1.call-start = ((), (), s32[]{:S(2)}) async-start(), calls=%async_computation.10 | async-start | bytes 2097152 | tf_op jit(solution)/shard_map/psum | solution.py:61
  626.9 12.9 copy-start.4
  652.8 99.1 %reduce-scatter.28.cloned.1.call-start = ((), (), s32[]{:S(2)}) async-start(), calls=%async_computation.25 | async-start | bytes 327680
  698.4 6.9 copy-start.11
  706.3 6.9 copy-start.11
  714.2 6.9 copy-start.11
  722.0 6.9 copy-start.11
  731.7 43.3 %reduce-scatter.30.cloned.1.call-start = ((), (), s32[]{:S(2)}) async-start(), calls=%async_computation.26 | async-start | bytes 327680
  731.8 12.8 copy-start.13
  745.4 100.6 %all-reduce.12.cloned.1.call-start = ((), (), s32[]{:S(2)}) async-start(), calls=%async_computation.27 | async-start | bytes 4194304 | tf_op jit(solution)/shard_map/psum | solution.py:61
  781.2 397.0 %reduce-scatter.26.cloned.1.call-start = ((), (), s32[]{:S(2)}) async-start(), calls=%async_computation.17 | async-start | bytes 35651584 | tf_op jit(solution)/shard_map/reduce_scatter | solution.py:349
  798.8 443.3 %reduce-scatter.16.cloned.1.call-start = ((), (), s32[]{:S(2)}) async-start(), calls=%async_computation.12 | async-start | bytes 2228224 | tf_op jit(solution)/shard_map/reduce_scatter | solution.py:344
  801.3 505.6 %reduce-scatter.18.cloned.1.call-start = ((), (), s32[]{:S(2)}) async-start(), calls=%async_computation.13 | async-start | bytes 2228224 | tf_op jit(solution)/shard_map/reduce_scatter | solution.py:345
  803.9 612.0 %reduce-scatter.14.cloned.1.call-start = ((), (), s32[]{:S(2)}) async-start(), calls=%async_computation.11 | async-start | bytes 8912896 | tf_op jit(solution)/shard_map/reduce_scatter | solution.py:343
  808.6 714.9 %reduce-scatter.20.cloned.1.call-start = ((), (), s32[]{:S(2)}) async-start(), calls=%async_computation.14 | async-start | bytes 8912896 | tf_op jit(solution)/shard_map/reduce_scatter | solution.py:346
  814.1 1043.5 %reduce-scatter.22.cloned.1.call-start = ((), (), s32[]{:S(2)}) async-start(), calls=%async_computation.15 | async-start | bytes 35651584 | tf_op jit(solution)/shard_map/reduce_scatter | solution.py:347
  829.4 1362.7 %reduce-scatter.24.cloned.1.call-start = ((), (), s32[]{:S(2)}) async-start(), calls=%async_computation.16 | async-start | bytes 35651584 | tf_op jit(solution)/shard_map/reduce_scatter | solution.py:348
  (11 other events, 23.6 us)
Sparse Core Ops, SparseCore 0:
  10.2 38.4 all-gather.16
  50.8 36.8 all-gather.18
  89.8 50.3 all-gather.20
  142.3 48.9 all-gather.22
  196.1 37.9 all-reduce.7
  236.1 125.2 all-gather.28
  363.6 124.5 all-gather.26
  490.4 124.5 all-gather.24
  652.9 39.4 all-reduce.9
  731.8 20.0 reduce-scatter.27
  754.9 20.0 reduce-scatter.29
  781.3 63.0 all-reduce.11
  848.6 329.5 reduce-scatter.25
  1182.4 59.6 reduce-scatter.15
  1246.2 60.7 reduce-scatter.17
  1311.4 104.4 reduce-scatter.13
  1420.4 103.0 reduce-scatter.19
  1528.2 329.3 reduce-scatter.21
  1862.5 329.6 reduce-scatter.23
where the time goes:
time: 2210 us; the launch traced here: 2200 us
  waiting for transfers between devices  1870 us (85%)
  matrix products  176 us (8%)
  blocking collectives  96.1 us (4%)
    reduce_scatter x1, waiting for transfers between devices, shards(): lax.psum_scatter(terms[7], ('dp', 'seq'), scatter_dimension=0, tiled=True)  334 us
    reduce_scatter x1, waiting for transfers between devices, shards(): lax.psum_scatter(terms[6], ('dp', 'seq'), scatter_dimension=0, tiled=True)  334 us
    reduce_scatter x1, waiting for transfers between devices, shards(): lax.psum_scatter(terms[8], ('dp', 'seq'), scatter_dimension=0, tiled=True)  278 us
    all_gather x1, waiting for transfers between devices, fetch(): lax.all_gather(w_down[layer_at], ('dp', 'seq'), axis=0, tiled=True)  126 us
    all_gather x1, waiting for transfers between devices, fetch(): lax.all_gather(w_gate[layer_at], ('dp', 'seq'), axis=0, tiled=True)  117 us
    all_gather x1, waiting for transfers between devices, fetch(): lax.all_gather(w_up[layer_at], ('dp', 'seq'), axis=0, tiled=True)  117 us
    reduce_scatter x1, waiting for transfers between devices, shards(): lax.psum_scatter(terms[2], ('dp', 'seq'), scatter_dimension=0, tiled=True)  109 us
    reduce_scatter x1, waiting for transfers between devices, shards(): lax.psum_scatter(terms[5], ('dp', 'seq'), scatter_dimension=0, tiled=True)  108 us
  transfers between devices with their start and end apart: 19, of which 18 were waited for; matrix products, arithmetic and copies ran while one was open for 6% of the time, Pallas kernels for 0%

commit v1 on v0

v1 whole, which is shorter than its diff:
```python
import functools

import jax
import jax.numpy as jnp
from jax import lax
from jax.experimental import pallas as pl
from jax.experimental.pallas import tpu as pltpu
from jax.sharding import PartitionSpec as P

HD = 64
MESH = pl.DeviceIdType.MESH

epsilon = 1e-05
rope_base = 500000.0


class Net:
    def __init__(self, send_sems, recv_sems):
        self.send_sems, self.recv_sems = send_sems, recv_sems
        self.copies = []

    def send(self, source, target, device):
        at = len(self.copies)
        copy = pltpu.make_async_remote_copy(
            src_ref=source,
            dst_ref=target,
            send_sem=self.send_sems.at[at],
            recv_sem=self.recv_sems.at[at],
            device_id=device,
            device_id_type=MESH,
        )
        copy.start()
        self.copies.append(copy)
        return copy

    def drain(self):
        for copy in self.copies:
            copy.wait_send()


def greet(devices):
    barrier = pltpu.get_barrier_semaphore()
    for device in devices:
        pl.semaphore_signal(barrier, inc=1, device_id=device, device_id_type=MESH)
    pl.semaphore_wait(barrier, len(devices))


def shifted(at, offset, size):
    return lax.rem(at + offset, size)


def call_kernel(body, inputs, outputs, in_vmem, copies, local, ident, name, scratch=()):
    spaces = [
        pl.BlockSpec(memory_space=pltpu.VMEM if inside else pl.ANY) for inside in in_vmem
    ]
    return pl.pallas_call(
        body,
        out_shape=outputs,
        in_specs=spaces,
        out_specs=[pl.BlockSpec(memory_space=pl.ANY)] * len(outputs),
        scratch_shapes=[
            pltpu.SemaphoreType.DMA((max(copies, 1),)),
            pltpu.SemaphoreType.DMA((max(copies, 1),)),
            pltpu.SemaphoreType.DMA((max(local, 1),)),
            *scratch,
        ],
        compiler_params=pltpu.CompilerParams(collective_id=ident, has_side_effects=True),
        name=name,
    )(*inputs)


def intake_kernel(sizes, pack_a, pack_f, piece, notes, all_a, all_f, pieces, all_notes, ssem, rsem, lsem):
    dp, seq, _ = sizes
    z, s = lax.axis_index("dp"), lax.axis_index("seq")
    mine = z * seq + s
    offsets = [(oz, os) for oz in range(dp) for os in range(seq) if oz or os]
    where = {o: (shifted(z, o[0], dp), shifted(s, o[1], seq)) for o in offsets}
    ids = {o: {"dp": where[o][0], "seq": where[o][1]} for o in offsets}
    greet([ids[o] for o in offsets])
    net = Net(ssem, rsem)
    for o in offsets:
        net.send(notes, all_notes.at[mine], ids[o])
    for o in offsets:
        net.send(pack_a.at[where[o][1]], all_a.at[mine], ids[o])
        if not o[0]:
            net.send(piece, pieces.at[s], ids[o])
    for o in offsets:
        net.send(pack_f.at[where[o][0] * seq + where[o][1]], all_f.at[mine], ids[o])
    own = [
        pltpu.make_async_copy(notes, all_notes.at[mine], lsem.at[0]),
        pltpu.make_async_copy(pack_a.at[s], all_a.at[mine], lsem.at[1]),
        pltpu.make_async_copy(piece, pieces.at[s], lsem.at[2]),
        pltpu.make_async_copy(pack_f.at[mine], all_f.at[mine], lsem.at[3]),
    ]
    for copy in own:
        copy.start()
    for copy in own:
        copy.wait()
    for copy in net.copies:
        copy.wait_recv()
    net.drain()


def intake(sizes, pack_a, pack_f, piece, notes, ident):
    dp, seq, _ = sizes
    n = dp * seq
    like = lambda lead, a: jax.ShapeDtypeStruct((lead,) + a.shape, a.dtype)
    return call_kernel(
        functools.partial(intake_kernel, sizes),
        (pack_a, pack_f, piece, notes),
        [
            jax.ShapeDtypeStruct((n,) + pack_a.shape[1:], pack_a.dtype),
            jax.ShapeDtypeStruct(pack_f.shape, pack_f.dtype),
            like(seq, piece),
            like(n, notes),
        ],
        [True] * 4,
        3 * (n - 1) + seq - 1,
        4,
        ident,
        "intake",
    )


def plane_sum_kernel(sizes, parts, landed, ssem, rsem, lsem):
    _, seq, ten = sizes
    s, t = lax.axis_index("seq"), lax.axis_index("tensor")
    offsets = [(os, ot) for os in range(seq) for ot in range(ten) if os or ot]
    where = {o: (shifted(s, o[0], seq), shifted(t, o[1], ten)) for o in offsets}
    ids = {o: {"seq": where[o][0], "tensor": where[o][1]} for o in offsets}
    greet([ids[o] for o in offsets])
    net = Net(ssem, rsem)
    for at, o in enumerate(offsets):
        net.send(parts.at[where[o][0], where[o][1]], landed.at[at], ids[o])
    for copy in net.copies:
        copy.wait_recv()
    net.drain()


def plane_sum(sizes, partial_rows, ident):
    _, seq, ten = sizes
    rows = partial_rows.shape[0] // (seq * ten)
    parts = partial_rows.reshape(seq, ten, rows, -1)
    (landed,) = call_kernel(
        functools.partial(plane_sum_kernel, sizes),
        (parts,),
        [jax.ShapeDtypeStruct((seq * ten - 1,) + parts.shape[2:], parts.dtype)],
        [False],
        seq * ten - 1,
        0,
        ident,
        "plane_sum",
    )
    own = parts[lax.axis_index("seq"), lax.axis_index("tensor")]
    return own.astype(jnp.float32) + jnp.sum(landed.astype(jnp.float32), axis=0)


def plane_gather_kernel(sizes, rows, whole, ssem, rsem, lsem):
    _, seq, ten = sizes
    s, t = lax.axis_index("seq"), lax.axis_index("tensor")
    offsets = [(os, ot) for os in range(seq) for ot in range(ten) if os or ot]
    ids = {
        o: {"seq": shifted(s, o[0], seq), "tensor": shifted(t, o[1], ten)} for o in offsets
    }
    greet([ids[o] for o in offsets])
    net = Net(ssem, rsem)
    for o in offsets:
        net.send(rows, whole.at[s, t], ids[o])
    own = pltpu.make_async_copy(rows, whole.at[s, t], lsem.at[0])
    own.start()
    own.wait()
    for copy in net.copies:
        copy.wait_recv()
    net.drain()


def plane_gather(sizes, rows, ident):
    _, seq, ten = sizes
    (whole,) = call_kernel(
        functools.partial(plane_gather_kernel, sizes),
        (rows,),
        [jax.ShapeDtypeStruct((seq, ten) + rows.shape, rows.dtype)],
        [True],
        seq * ten - 1,
        1,
        ident,
        "plane_gather",
    )
    return whole.reshape(-1, rows.shape[-1])


def full_gather_kernel(sizes, rows, whole, ssem, rsem, lsem):
    dp, seq, ten = sizes
    inner = whole.shape[2]
    outer = seq // inner
    z, s, t = lax.axis_index("dp"), lax.axis_index("seq"), lax.axis_index("tensor")
    y, c = lax.div(s, inner), lax.rem(s, inner)
    half = rows.shape[-1] // 2
    front, back = pl.ds(0, half), pl.ds(half, half)
    to_dp = [{"dp": shifted(z, o, dp)} for o in range(1, dp)]
    to_ten = [{"tensor": shifted(t, o, ten)} for o in range(1, ten)]
    to_outer = [{"seq": shifted(y, o, outer) * inner + c} for o in range(1, outer)]
    to_inner = [{"seq": y * inner + shifted(c, o, inner)} for o in range(1, inner)]
    greet(to_dp + to_ten + to_outer + to_inner)
    net = Net(ssem, rsem)
    own = pltpu.make_async_copy(rows, whole.at[z, y, c, t], lsem.at[0])
    own.start()
    first = [net.send(rows, whole.at[z, y, c, t], device) for device in to_dp]
    came = [shifted(z, dp - k, dp) for k in range(dp)]
    second, third, fourth = {}, {}, {}
    for step in range(dp + 3):
        if step < dp:
            k = step
            if k:
                first[k - 1].wait_recv()
            block = rows if k == 0 else whole.at[came[k], y, c, t]
            there = whole.at[came[k], y, c, t]
            second[k] = [
                net.send(block.at[:, front], there.at[:, front], device) for device in to_ten
            ] + [net.send(block.at[:, back], there.at[:, back], device) for device in to_outer]
        if step == 0:
            own.wait()
        if 0 <= step - 1 < dp:
            k = step - 1
            for copy in second[k]:
                copy.wait_recv()
            strip = whole.at[came[k], y, c, :, :, front]
            stack = whole.at[came[k], :, c, t, :, back]
            third[k] = [net.send(strip, strip, device) for device in to_outer] + [
                net.send(stack, stack, device) for device in to_ten
            ]
        if 0 <= step - 2 < dp:
            k = step - 2
            for copy in third[k]:
                copy.wait_recv()
            side = whole.at[came[k], :, c]
            fourth[k] = [net.send(side, side, device) for device in to_inner]
        if 0 <= step - 3 < dp:
            for copy in fourth[step - 3]:
                copy.wait_recv()
    net.drain()


def full_gather(sizes, rows, ident):
    dp, seq, ten = sizes
    inner = 2 if seq % 2 == 0 else 1
    outer = seq // inner
    copies = dp - 1 + dp * (2 * (ten - 1) + 2 * (outer - 1) + inner - 1)
    (whole,) = call_kernel(
        functools.partial(full_gather_kernel, sizes),
        (rows,),
        [jax.ShapeDtypeStruct((dp, outer, inner, ten) + rows.shape, rows.dtype)],
        [True],
        copies,
        1,
        ident,
        "full_gather",
    )
    return whole.reshape(-1, rows.shape[-1])


def outtake_kernel(
    sizes, grad_a, grad_f, gains, row_grad, row_out, all_a, all_f, all_gains, pair_grad, pair_out,
    ssem, rsem, lsem,
):
    dp, seq, ten = sizes
    z, s, t = lax.axis_index("dp"), lax.axis_index("seq"), lax.axis_index("tensor")
    mine = z * seq + s
    offsets = [
        (oz, os, ot)
        for oz in range(dp)
        for os in range(seq)
        for ot in range(ten)
        if oz or os or ot
    ]
    where = {
        o: (shifted(z, o[0], dp), shifted(s, o[1], seq), shifted(t, o[2], ten)) for o in offsets
    }
    ids = {o: {"dp": where[o][0], "seq": where[o][1], "tensor": where[o][2]} for o in offsets}
    greet([ids[o] for o in offsets])
    net = Net(ssem, rsem)
    for o in offsets:
        owner = where[o][0] * seq + where[o][1]
        net.send(gains.at[owner], all_gains.at[z, s, t], ids[o])
        if o[2] == 0:
            net.send(grad_a.at[owner], all_a.at[mine], ids[o])
            net.send(grad_f.at[owner], all_f.at[mine], ids[o])
        if o[0] == 0 and o[1] == 0:
            net.send(row_grad, pair_grad.at[t], ids[o])
            net.send(row_out, pair_out.at[t], ids[o])
    own = [
        pltpu.make_async_copy(grad_a.at[mine], all_a.at[mine], lsem.at[0]),
        pltpu.make_async_copy(grad_f.at[mine], all_f.at[mine], lsem.at[1]),
        pltpu.make_async_copy(gains.at[mine], all_gains.at[z, s, t], lsem.at[2]),
        pltpu.make_async_copy(row_grad, pair_grad.at[t], lsem.at[3]),
        pltpu.make_async_copy(row_out, pair_out.at[t], lsem.at[4]),
    ]
    for copy in own:
        copy.start()
    for copy in own:
        copy.wait()
    for copy in net.copies:
        copy.wait_recv()
    net.drain()


def outtake(sizes, grad_a, grad_f, gains, row_grad, row_out, ident):
    dp, seq, ten = sizes
    n = dp * seq
    return call_kernel(
        functools.partial(outtake_kernel, sizes),
        (grad_a, grad_f, gains, row_grad, row_out),
        [
            jax.ShapeDtypeStruct(grad_a.shape, grad_a.dtype),
            jax.ShapeDtypeStruct(grad_f.shape, grad_f.dtype),
            jax.ShapeDtypeStruct((dp, seq, ten) + gains.shape[1:], gains.dtype),
            jax.ShapeDtypeStruct((ten,) + row_grad.shape, row_grad.dtype),
            jax.ShapeDtypeStruct((ten,) + row_out.shape, row_out.dtype),
        ],
        [True] * 5,
        n * ten - 1 + 2 * (n - 1) + 2 * (ten - 1),
        5,
        ident,
        "outtake",
    )


def full_sum(partial_rows):
    return lax.psum_scatter(
        partial_rows, ("dp", "seq", "tensor"), scatter_dimension=0, tiled=True
    ).astype(jnp.float32)


def norm_forward(stream, gain):
    inverse = lax.rsqrt(jnp.mean(stream * stream, axis=-1, keepdims=True) + epsilon)
    return ((stream * inverse * gain).astype(jnp.bfloat16), inverse)


def norm_backward(stream, inverse, gain, normed_grad):
    unit_rms = stream * inverse
    gain_grad = jnp.sum(normed_grad * unit_rms, axis=0)
    scaled = normed_grad * gain
    return (
        inverse * (scaled - unit_rms * jnp.mean(scaled * unit_rms, axis=-1, keepdims=True)),
        gain_grad,
    )


def rope_tables(position, head_dim):
    half_dim = head_dim // 2
    frequency = rope_base ** (-jnp.arange(half_dim, dtype=jnp.float32) / half_dim)
    angles = position[:, None] * frequency[None, :]
    return (jnp.cos(angles)[:, None, :], jnp.sin(angles)[:, None, :])


def rotate(values, cosine, sine_table, direction):
    half_dim = values.shape[-1] // 2
    first_half = values[..., :half_dim]
    second_half = values[..., half_dim:]
    return jnp.concatenate(
        [
            first_half * cosine - direction * second_half * sine_table,
            second_half * cosine + direction * first_half * sine_table,
        ],
        axis=-1,
    )


def dot(left, right):
    return jnp.dot(left, right, preferred_element_type=jnp.float32)


def dot_last(left, right):
    return lax.dot_general(
        left, right, (((1,), (1,)), ((), ())), preferred_element_type=jnp.float32
    )


def dot_rows(left, right):
    return lax.dot_general(
        left, right, (((0,), (0,)), ((), ())), preferred_element_type=jnp.float32
    )


def product(spec, left, right):
    return jnp.einsum(spec, left, right, preferred_element_type=jnp.float32)


def shards(
    sizes,
    tokens,
    positions,
    gain_attn,
    gain_ffn,
    w_query,
    w_key,
    w_value,
    w_out,
    w_gate,
    w_up,
    w_down,
    cotangent,
):
    dp, seq, ten = sizes
    n = dp * seq
    bf = jnp.bfloat16
    piece, width = tokens.shape[1:]
    band = w_query.shape[1]
    rows = piece // ten
    length = piece * seq
    s, t = lax.axis_index("seq"), lax.axis_index("tensor")

    q_cols = w_query.shape[2] // seq
    kv_local = w_key.shape[2] // HD
    repeat = max(1, seq // kv_local)
    k_cols = w_key.shape[2] * repeat // seq
    heads, groups = q_cols // HD, k_cols // HD
    per_group = heads // groups
    f_cols = w_gate.shape[2] // n

    def by_seq(weight, cols):
        return jnp.moveaxis(weight.reshape(band, -1, cols), 1, 0)

    pack_a = jnp.concatenate(
        [
            by_seq(w_query[0], q_cols),
            jnp.repeat(by_seq(w_key[0], k_cols), repeat, axis=0),
            jnp.repeat(by_seq(w_value[0], k_cols), repeat, axis=0),
            by_seq(w_out[0], q_cols),
        ],
        axis=-1,
    )
    pack_f = jnp.concatenate([by_seq(w[0], f_cols) for w in (w_gate, w_up, w_down)], axis=-1)
    span = -(-max(piece, band) // 128) * 128

    def note(values):
        values = values.reshape(1, -1).astype(jnp.float32)
        return jnp.pad(values, ((0, 7), (0, span - values.shape[1])))

    notes = jnp.concatenate([note(gain_attn), note(gain_ffn), note(positions)], axis=0)
    all_cotangent = lax.all_gather(cotangent[0], ("dp", "seq"), axis=0, tiled=True)
    all_a, all_f, pieces, all_notes = intake(sizes, pack_a, pack_f, tokens[0], notes, 0)
    gain_one = all_notes[:, 0, :band].reshape(1, width)
    gain_two = all_notes[:, 8, :band].reshape(1, width)
    z = lax.axis_index("dp")
    position = lax.dynamic_slice_in_dim(all_notes[:, 16, :piece], z * seq, seq, 0).reshape(length)
    all_a = all_a.reshape(width, -1)
    all_f = all_f.reshape(width, -1)
    w_qkv, w_o = all_a[:, : q_cols + 2 * k_cols], all_a[:, q_cols + 2 * k_cols :]
    w_gu, w_d = all_f[:, : 2 * f_cols], all_f[:, 2 * f_cols :]

    def own_rows(whole_piece):
        return lax.dynamic_slice_in_dim(whole_piece, t * rows, rows, 0)

    cosine, sine = rope_tables(position, HD)
    stream = pieces.reshape(length, width).astype(jnp.float32)
    normed_one, _ = norm_forward(stream, gain_one)
    qkv = dot(normed_one, w_qkv)
    queries = rotate(qkv[:, :q_cols].reshape(length, heads, HD), cosine, sine, 1.0).astype(bf)
    keys = rotate(
        qkv[:, q_cols : q_cols + k_cols].reshape(length, groups, HD), cosine, sine, 1.0
    ).astype(bf)
    values = qkv[:, q_cols + k_cols :].reshape(length, groups, HD).astype(bf)
    queries = queries.reshape(length, groups, per_group, HD)
    scale = HD**-0.5
    scores = product("qngd,knd->ngqk", queries, keys) * scale
    index = jnp.arange(length, dtype=jnp.int32)
    scores = jnp.where(index[:, None] >= index[None, :], scores, -1e30)
    exps = jnp.exp(scores - jnp.max(scores, axis=-1, keepdims=True))
    probability = exps / jnp.sum(exps, axis=-1, keepdims=True)
    low_probability = probability.astype(bf)
    attended = product("ngqk,knd->qngd", low_probability, values).astype(bf)
    flat_attended = attended.reshape(length, q_cols)
    mixed = plane_sum(sizes, dot_last(flat_attended, w_o).astype(bf), 1)
    row_stream = own_rows(tokens[0]).astype(jnp.float32)
    after_attn = row_stream + mixed

    row_normed, inverse_two = norm_forward(after_attn, gain_two)
    normed_two = full_gather(sizes, row_normed, 2)
    gate_up = dot(normed_two, w_gu)
    gate, up = gate_up[:, :f_cols], gate_up[:, f_cols:]
    sigmoid_gate = jax.nn.sigmoid(gate)
    hidden = (gate * sigmoid_gate * up).astype(bf)
    hidden_grad = dot(all_cotangent, w_d)
    gate_grad = (hidden_grad * up * sigmoid_gate * (1.0 + gate * (1.0 - sigmoid_gate))).astype(bf)
    up_grad = (hidden_grad * gate * sigmoid_gate).astype(bf)
    gu_grad = jnp.concatenate([gate_grad, up_grad], axis=-1)
    normed_two_grad = full_sum(dot_last(gu_grad, w_gu).astype(bf))
    row_out = after_attn + full_sum(dot_last(hidden, w_d).astype(bf))
    grad_f = jnp.concatenate(
        [dot_rows(normed_two, gu_grad), dot_rows(all_cotangent, hidden)], axis=-1
    ).astype(bf)

    row_cotangent = own_rows(cotangent[0]).astype(jnp.float32)
    part, gain_two_grad = norm_backward(after_attn, inverse_two, gain_two, normed_two_grad)
    resid_grad = row_cotangent + part

    resid_low = plane_gather(sizes, resid_grad.astype(bf), 3)
    attended_grad = dot(resid_low, w_o).astype(bf).reshape(attended.shape)
    value_grad = product("ngqk,qngd->knd", low_probability, attended_grad)
    prob_grad = product("qngd,knd->ngqk", attended_grad, values)
    row_dots = jnp.sum(attended_grad.astype(jnp.float32) * attended.astype(jnp.float32), axis=-1)
    score_grad = (
        probability * (prob_grad - jnp.moveaxis(row_dots, 0, -1)[..., None]) * scale
    ).astype(bf)
    query_grad = product("ngqk,knd->qngd", score_grad, keys).reshape(length, heads, HD)
    key_grad = product("ngqk,qngd->knd", score_grad, queries)
    qkv_grad = jnp.concatenate(
        [
            rotate(query_grad, cosine, sine, -1.0).reshape(length, q_cols),
            rotate(key_grad, cosine, sine, -1.0).reshape(length, k_cols),
            value_grad.reshape(length, k_cols),
        ],
        axis=-1,
    ).astype(bf)
    grad_a = jnp.concatenate(
        [dot_rows(normed_one, qkv_grad), dot_rows(resid_low, flat_attended)], axis=-1
    ).astype(bf)
    normed_one_grad = plane_sum(sizes, dot_last(qkv_grad, w_qkv).astype(bf), 4)
    inverse_one = lax.rsqrt(jnp.mean(row_stream * row_stream, axis=-1, keepdims=True) + epsilon)
    part, gain_one_grad = norm_backward(row_stream, inverse_one, gain_one, normed_one_grad)
    row_grad = resid_grad + part

    gains = jnp.pad(jnp.stack([gain_one_grad, gain_two_grad]), ((0, 6), (0, 0)))
    gains = jnp.moveaxis(gains.reshape(8, n, band), 1, 0)
    got_a, got_f, got_gains, pair_grad, pair_out = outtake(
        sizes,
        grad_a.reshape(n, band, -1),
        grad_f.reshape(n, band, -1),
        gains,
        row_grad,
        row_out.astype(bf),
        5,
    )
    got_a = jnp.sum(got_a.reshape(dp, seq, band, -1).astype(jnp.float32), axis=0)
    got_f = got_f.astype(jnp.float32)
    got_gains = jnp.sum(got_gains, axis=(0, 1, 2))

    def spread(block):
        return jnp.moveaxis(block, 0, 1).reshape(1, band, -1)

    def shared(block):
        return spread(jnp.sum(block.reshape(seq // repeat, repeat, band, k_cols), axis=1))

    return (
        pair_out.reshape(1, piece, width),
        pair_grad.reshape(1, piece, width),
        got_gains[0:1],
        got_gains[1:2],
        spread(got_a[..., :q_cols]),
        shared(got_a[..., q_cols : q_cols + k_cols]),
        shared(got_a[..., q_cols + k_cols : q_cols + 2 * k_cols]),
        spread(got_a[..., q_cols + 2 * k_cols :]),
        spread(got_f[..., :f_cols]),
        spread(got_f[..., f_cols : 2 * f_cols]),
        spread(got_f[..., 2 * f_cols :]),
    )


def solution(mesh):
    weight = P(None, ("dp", "seq"), "tensor")
    gain = P(None, ("dp", "seq"))
    rows = P("dp", "seq", None)
    in_specs = (rows, P("dp", "seq"), gain, gain) + (weight,) * 7 + (rows,)
    out_specs = (rows, rows, gain, gain) + (weight,) * 7
    sizes = (mesh.shape["dp"], mesh.shape["seq"], mesh.shape["tensor"])
    return jax.shard_map(
        functools.partial(shards, sizes),
        mesh=mesh,
        in_specs=in_specs,
        out_specs=out_specs,
        check_vma=False,
    )
```

time: 2210 us -> 970 us (0.44)
  waiting for transfers between devices: 1870 us -> 336 us
  Pallas kernels: 0 us -> 441 us
  matrix products: 176 us -> 73.8 us
  blocking collectives: 96.1 us -> 0 us
  local copies, waits for them, and re-layouts: 21.3 us -> 66.2 us
    reduce_scatter x7 -> x2, waiting for transfers between devices: 1290 us -> 335 us  [full_sum(): lax.psum_scatter(partial_rows, ('dp', 'seq', 'tensor'), scatter_dimension...]
    all_gather x7 -> x1, waiting for transfers between devices: 490 us -> 0.01 us  [shards(): lax.all_gather(cotangent[0], ('dp', 'seq'), axis=0, tiled=True)]
    pallas_call x0 -> x6, Pallas kernels: none -> 441 us  [call_kernel(): pl.pallas_call(body, out_shape=outputs, in_specs=spaces, out_specs=[pl.Bl...]
    dot_general x49 -> x18, matrix products: 176 us -> 73.8 us  [the longest x4 23.8 us: dot(): return jnp.dot(left, right, preferred_element_type=jnp.float32)]
    psum x3 -> x0, waiting for transfers between devices: 59.1 us -> none  [tensor_sum(): return lax.psum(partial_sum, 'tensor')]
    unnamed x1 -> x0, blocking collectives: 48.3 us -> none
    all_gather x4 -> x0, blocking collectives: 47.8 us -> none  [the longest x1 19.5 us: fetch(): lax.all_gather(gain_attn[layer_at], ('dp', 'seq'), axis=0, tiled=True)]
    unnamed x21 -> x3, waiting for transfers between devices: 31.7 us -> 0.71 us
  transfers between devices with their start and end apart: 19 -> 3, of which waited for: 18 -> 2; matrix products, arithmetic and copies ran while one was open for 6% -> 9% of each run, Pallas kernels for 0% -> 26%
where the time goes in v1:
time: 970 us; the launch traced here: 966 us
  Pallas kernels  441 us (45%)
  waiting for transfers between devices  336 us (35%)
  matrix products  73.8 us (8%)
  local copies, waits for them, and re-layouts  66.2 us (7%)
  other arithmetic  34.2 us (4%)
  between operations  14.8 us (2%)
    pallas_call x6, Pallas kernels, call_kernel(): pl.pallas_call(body, out_shape=outputs, in_specs=spaces, out_specs=[pl.Bl...  441 us
    reduce_scatter x2, waiting for transfers between devices, full_sum(): lax.psum_scatter(partial_rows, ('dp', 'seq', 'tensor'), scatter_dimension...  335 us
    dot_general x4, matrix products, dot(): return jnp.dot(left, right, preferred_element_type=jnp.float32)  23.8 us
    unnamed x114, local copies, waits for them, and re-layouts  23.7 us
    dot_general x4, matrix products, dot_last(): lax.dot_general(left, right, (((1,), (1,)), ((), ())), preferred_element_...  21.5 us
  transfers between devices with their start and end apart: 3, of which 2 were waited for; matrix products, arithmetic and copies ran while one was open for 9% of the time, Pallas kernels for 26%

profile of v1, /device:TPU:9, one launch (start us, length us, event | category | flops | bytes accessed | tf_op | source)
XLA Modules:
  0.0 965.9 jit_solution(14402155310809180487)
XLA Ops:
  22.8 3.0 pad_maximum_fusion.pack_f
  25.8 177.2 %intake.1 = (bf16[16,128,640]{2,1,0:T(8,128)(2,1)}, bf16[16,128,768]{2,1,0:T(8,128)(2,1)}, bf16[4,128,2048]{2,1,0:T(8,128)(2,1)}, f32[16,24,128]{2,1,0:T(8,128)}) custom-call(bf16[4,128,640]{2,1,0:T(8,128)(2,1)} %pad_maximum_fusion.6.pack_a, bf16[16,128,768]{2,1,0:T(8,128)(2,1)} %pad_maximum_fusion.pack_f, bf16[128,2048]{1,0:T(8,128)(2,1)} %bitcast.267, ...), custom_call_target="tpu_custom_call" | custom-call | tf_op jit(solution)/shard_map/intake/pallas_call | solution.py:56
  203.0 2.2 multiply_reduce_fusion
  212.6 2.4 fusion.44
  215.0 3.3 convolution_convert_fusion.2
  218.4 26.3 %plane_sum.2 = bf16[7,64,2048]{2,1,0:T(8,128)(2,1)} custom-call(bf16[4,2,64,2048]{3,2,1,0:T(8,128)(2,1)} %bitcast.250), custom_call_target="tpu_custom_call" | custom-call | tf_op jit(solution)/shard_map/plane_sum/pallas_call | solution.py:56
  249.1 46.9 %full_gather.1 = bf16[4,2,2,2,64,2048]{5,4,3,2,1,0:T(8,128)(2,1)} custom-call(bf16[64,2048]{1,0:T(8,128)(2,1)} %multiply_convert_fusion.3.rows), custom_call_target="tpu_custom_call" | custom-call | tf_op jit(solution)/shard_map/full_gather/pallas_call | solution.py:56
  296.0 10.9 %fusion.36 = f32[2048,512]{0,1:T(8,128)} fusion(bf16[2048,2048]{1,0:T(8,128)(2,1)} %bitcast.248, bf16[2048,768]{1,0:T(8,128)(2,1)} %bitcast.293), kind=kOutput, calls=%fused_computation.51 | convolution fusion | flops 4294967296 | bytes 14680064 | tf_op jit(solution)/shard_map/dot_general | solution.py:370
  306.8 9.2 multiply_convert_fusion.2
  317.3 7.0 convolution_convert_fusion.1
  324.4 7.2 convolution_convert_fusion
  331.6 2.5 copy.124
  334.1 12.4 %copy.134 = bf16[2048,2048]{1,0:T(8,128)(2,1)} copy(bf16[2048,2048]{0,1:T(8,128)(2,1)} %bitcast.249) | data formatting | bytes 16777216 | tf_op jit(solution)/shard_map/dot_general | solution.py:380
  347.1 5.8 fusion.18
  353.8 8.5 fusion.32
  364.2 150.3 %reduce-scatter.3.cloned.1.call-done = bf16[64,2048]{1,0:T(8,128)(2,1)} async-done(((bf16[2048,2048]{1,0:T(8,128)(2,1)}), bf16[64,2048]{1,0:T(8,128)(2,1)}) %reduce-scatter.3.cloned.1.call-update) | async-done | bytes 262160 | tf_op jit(solution)/shard_map/reduce_scatter | solution.py:329
  516.2 184.6 %reduce-scatter.5.cloned.1.call-done = bf16[64,2048]{1,0:T(8,128)(2,1)} async-done(((bf16[2048,2048]{1,0:T(8,128)(2,1)}), bf16[64,2048]{1,0:T(8,128)(2,1)}) %reduce-scatter.5.cloned.1.call-update) | async-done | bytes 262160 | tf_op jit(solution)/shard_map/reduce_scatter | solution.py:329
  702.9 28.9 %plane_gather.1 = bf16[4,2,64,2048]{3,2,1,0:T(8,128)(2,1)} custom-call(bf16[64,2048]{1,0:T(8,128)(2,1)} %get-tuple-element.83.rows), custom_call_target="tpu_custom_call" | custom-call | tf_op jit(solution)/shard_map/plane_gather/pallas_call | solution.py:56
  731.8 2.8 convolution_convert_fusion.6
  736.9 2.7 fusion.6
  744.1 4.0 convolution_convert_fusion.3
  748.2 2.7 convolution_convert_fusion.4
  750.8 26.3 %plane_sum.3 = bf16[7,64,2048]{2,1,0:T(8,128)(2,1)} custom-call(bf16[4,2,64,2048]{3,2,1,0:T(8,128)(2,1)} %bitcast.268), custom_call_target="tpu_custom_call" | custom-call | tf_op jit(solution)/shard_map/plane_sum/pallas_call | solution.py:56
  780.4 2.5 copy.132
  783.5 2.3 convolution_convert_fusion.5
  787.8 2.2 fusion.76.row_grad
  789.9 135.7 %outtake.1 = (bf16[16,128,640]{2,1,0:T(8,128)(2,1)}, bf16[16,128,768]{2,1,0:T(8,128)(2,1)}, f32[4,4,2,8,128]{4,3,2,1,0:T(8,128)}, f32[2,64,2048]{2,1,0:T(8,128)}, bf16[2,64,2048]{2,1,0:T(8,128)(2,1)}) custom-call(bf16[16,128,640]{2,1,0:T(8,128)(2,1)} %pad_maximum_fusion.2.grad_a, bf16[16,128,768]{2,1,0:T(8,128)(2,1)} %pad_maximum_fusion.1.grad_f, ...), custom_call_target="tpu_custom_call" | custom-call | tf_op jit(solution)/shard_map/outtake/pallas_call | solution.py:56
  925.6 2.3 convert_reduce_fusion
  930.4 2.3 copy.140
  932.7 2.0 copy.147
  939.5 2.0 copy.144
  942.2 2.9 slice_bitcast_fusion
  (181 shorter events, 69.9 us)
Async XLA Ops:
  7.2 7.6 copy-start.15
  7.2 299.7 %all-gather.3.cloned.1.call-start = ((), (), s32[]{:S(2)}) async-start(), calls=%async_computation.4 | async-start | bytes 8912896 | tf_op jit(solution)/shard_map/all_gather | solution.py:441
  7.9 506.6 %reduce-scatter.3.cloned.1.call-start = ((), (), s32[]{:S(2)}) async-start(), calls=%async_computation.2 | async-start | bytes 8650752 | tf_op jit(solution)/shard_map/reduce_scatter | solution.py:329
  11.5 4.6 copy-start.16
  16.7 3.5 copy-start.45
  16.7 3.5 copy-start.46
  203.0 3.2 copy-start.1
  203.0 3.7 copy-start.23
  208.9 3.7 copy-start.13
  211.6 3.4 copy-start.2
  211.6 3.4 copy-start.33
  218.4 28.2 %copy-start.4 = (bf16[1,128,2048]{2,1,0:T(8,128)(2,1)S(1)}, bf16[1,128,2048]{2,1,0:T(8,128)(2,1)}, u32[]{:S(2)}) copy-start(bf16[1,128,2048]{2,1,0:T(8,128)(2,1)} %param.12) | copy-start | bytes 1572868
  248.3 452.6 %copy-start.37 = (f32[64]{0:T(128)}, f32[64]{0:T(128)S(1)}, u32[]{:S(2)}) copy-start(f32[64]{0:T(128)S(1)} %add_rsqrt_fusion.1) | copy-start | bytes 772
  306.8 10.5 %copy-start.24 = (bf16[16,128,768]{2,1,0:T(8,128)(2,1)S(1)}, bf16[16,128,768]{2,1,0:T(8,128)(2,1)}, u32[]{:S(2)}) copy-start(bf16[16,128,768]{2,1,0:T(8,128)(2,1)} %get-tuple-element.23) | copy-start | bytes 9437188
  324.3 376.5 %reduce-scatter.5.cloned.1.call-start = ((), (), s32[]{:S(2)}) async-start(), calls=%async_computation.3 | async-start | bytes 8650752 | tf_op jit(solution)/shard_map/reduce_scatter | solution.py:329
  334.1 12.5 %copy-start.44 = (f32[64]{0:T(128)S(1)}, f32[64]{0:T(128)}, u32[]{:S(2)}) copy-start(f32[64]{0:T(128)} %get-tuple-element.84) | copy-start | bytes 772
  334.1 13.0 %copy-start.11 = (bf16[2048,256]{0,1:T(8,128)(2,1)S(1)}, bf16[2048,256]{0,1:T(8,128)(2,1)}, u32[]{:S(2)}) copy-start(bf16[2048,256]{0,1:T(8,128)(2,1)} %get-tuple-element.73) | copy-start | bytes 3145732
  362.3 338.6 %copy-start.9 = (bf16[1,128,2048]{2,1,0:T(8,128)(2,1)S(1)}, bf16[1,128,2048]{2,1,0:T(8,128)(2,1)}, u32[]{:S(2)}) copy-start(bf16[1,128,2048]{2,1,0:T(8,128)(2,1)} %param.23) | copy-start | bytes 1572868
  516.2 218.3 %copy-start.42 = (f32[64]{0:T(128)}, f32[64]{0:T(128)S(1)}, u32[]{:S(2)}) copy-start(f32[64]{0:T(128)S(1)} %broadcast_multiply_fusion.2) | copy-start | bytes 772
  702.9 31.8 %copy-start.14 = (pred[512,512]{0,1:T(8,128)(4,1)S(1)}, pred[512,512]{0,1:T(8,128)(4,1)}, u32[]{:S(2)}) copy-start(pred[512,512]{0,1:T(8,128)(4,1)} %copy-done.13) | copy-start | bytes 786436
  702.9 31.8 %copy-start.34 = (f32[4,512]{1,0:T(4,128)S(1)}, f32[4,512]{1,0:T(4,128)}, u32[]{:S(2)}) copy-start(f32[4,512]{1,0:T(4,128)} %copy-done.33) | copy-start | bytes 24580
  702.9 31.8 %copy-start.36 = (f32[4,512]{1,0:T(4,128)S(1)}, f32[4,512]{1,0:T(4,128)}, u32[]{:S(2)}) copy-start(f32[4,512]{1,0:T(4,128)} %copy-done.35) | copy-start | bytes 24580
  731.8 3.2 copy-start.3
  736.9 3.5 copy-start.26
  736.9 3.5 copy-start.28
  742.0 6.2 copy-start.8
  750.8 28.2 %copy-start.41 = (f32[64]{0:T(128)S(1)}, f32[64]{0:T(128)}, u32[]{:S(2)}) copy-start(f32[64]{0:T(128)} %add_rsqrt_fusion) | copy-start | bytes 772
  750.8 29.5 %copy-start = (bf16[4,2,64,2048]{3,2,1,0:T(8,128)(2,1)S(1)}, bf16[4,2,64,2048]{3,2,1,0:T(8,128)(2,1)}, u32[]{:S(2)}) copy-start(bf16[4,2,64,2048]{3,2,1,0:T(8,128)(2,1)} %plane_gather.1) | copy-start | bytes 6291460
  779.0 3.9 copy-start.32
  925.6 4.2 copy-start.29
  929.8 11.7 %copy-start.6 = (bf16[16,128,768]{2,1,0:T(8,128)(2,1)S(1)}, bf16[16,128,768]{2,1,0:T(8,128)(2,1)}, u32[]{:S(2)}) copy-start(bf16[16,128,768]{2,1,0:T(8,128)(2,1)} %get-tuple-element.28) | copy-start | bytes 9437188
  954.5 3.7 copy-start.17
  (20 other events, 38.3 us)
Sparse Core Ops, SparseCore 0:
  10.2 159.3 all-gather.2
  324.4 190.0 reduce-scatter.2
  516.8 183.9 reduce-scatter.4

commit v2 on v1

--- a/solution.py
+++ b/solution.py
@@ -6,6 +6,7 @@
 from jax.experimental import pallas as pl
 from jax.experimental.pallas import tpu as pltpu
 from jax.sharding import PartitionSpec as P
+
 
 HD = 64
 MESH = pl.DeviceIdType.MESH
@@ -49,7 +50,7 @@
     return lax.rem(at + offset, size)
 
 
-def call_kernel(body, inputs, outputs, in_vmem, copies, local, ident, name, scratch=()):
+def call_kernel(body, inputs, outputs, in_vmem, copies, local, ident, scratch=()):
     spaces = [
         pl.BlockSpec(memory_space=pltpu.VMEM if inside else pl.ANY) for inside in in_vmem
     ]
@@ -65,11 +66,13 @@
             *scratch,
         ],
         compiler_params=pltpu.CompilerParams(collective_id=ident, has_side_effects=True),
-        name=name,
+        cost_estimate=pl.CostEstimate(
+            flops=0, bytes_accessed=40 * sum(a.size * a.dtype.itemsize for a in inputs), transcendentals=0
+        ),
     )(*inputs)
 
 
-def intake_kernel(sizes, pack_a, pack_f, piece, notes, all_a, all_f, pieces, all_notes, ssem, rsem, lsem):
+def intake_kernel(sizes, pack_a, pack_f, piece, notes, all_a, staged_f, pieces, all_notes, ssem, rsem, lsem):
     dp, seq, _ = sizes
     z, s = lax.axis_index("dp"), lax.axis_index("seq")
     mine = z * seq + s
@@ -85,12 +88,13 @@
         if not o[0]:
             net.send(piece, pieces.at[s], ids[o])
     for o in offsets:
-        net.send(pack_f.at[where[o][0] * seq + where[o][1]], all_f.at[mine], ids[o])
+        if not o[0]:
+            net.send(pack_f.at[:, where[o][1]], staged_f.at[:, s], ids[o])
     own = [
         pltpu.make_async_copy(notes, all_notes.at[mine], lsem.at[0]),
         pltpu.make_async_copy(pack_a.at[s], all_a.at[mine], lsem.at[1]),
         pltpu.make_async_copy(piece, pieces.at[s], lsem.at[2]),
-        pltpu.make_async_copy(pack_f.at[mine], all_f.at[mine], lsem.at[3]),
+        pltpu.make_async_copy(pack_f.at[:, s], staged_f.at[:, s], lsem.at[3]),
     ]
     for copy in own:
         copy.start()
@@ -115,10 +119,9 @@
             like(n, notes),
         ],
         [True] * 4,
-        3 * (n - 1) + seq - 1,
+        2 * (n - 1) + 2 * (seq - 1),
         4,
         ident,
-        "intake",
     )
 
 
@@ -149,7 +152,6 @@
         seq * ten - 1,
         0,
         ident,
-        "plane_sum",
     )
     own = parts[lax.axis_index("seq"), lax.axis_index("tensor")]
     return own.astype(jnp.float32) + jnp.sum(landed.astype(jnp.float32), axis=0)
@@ -184,7 +186,6 @@
         seq * ten - 1,
         1,
         ident,
-        "plane_gather",
     )
     return whole.reshape(-1, rows.shape[-1])
 
@@ -254,7 +255,6 @@
         copies,
         1,
         ident,
-        "full_gather",
     )
     return whole.reshape(-1, rows.shape[-1])
 
@@ -284,13 +284,14 @@
         net.send(gains.at[owner], all_gains.at[z, s, t], ids[o])
         if o[2] == 0:
             net.send(grad_a.at[owner], all_a.at[mine], ids[o])
-            net.send(grad_f.at[owner], all_f.at[mine], ids[o])
+        if o[0] == 0 and o[2] == 0:
+            net.send(grad_f.at[:, where[o][1]], all_f.at[:, s], ids[o])
         if o[0] == 0 and o[1] == 0:
             net.send(row_grad, pair_grad.at[t], ids[o])
             net.send(row_out, pair_out.at[t], ids[o])
     own = [
         pltpu.make_async_copy(grad_a.at[mine], all_a.at[mine], lsem.at[0]),
-        pltpu.make_async_copy(grad_f.at[mine], all_f.at[mine], lsem.at[1]),
+        pltpu.make_async_copy(grad_f.at[:, s], all_f.at[:, s], lsem.at[1]),
         pltpu.make_async_copy(gains.at[mine], all_gains.at[z, s, t], lsem.at[2]),
         pltpu.make_async_copy(row_grad, pair_grad.at[t], lsem.at[3]),
         pltpu.make_async_copy(row_out, pair_out.at[t], lsem.at[4]),
@@ -318,17 +319,155 @@
             jax.ShapeDtypeStruct((ten,) + row_out.shape, row_out.dtype),
         ],
         [True] * 5,
-        n * ten - 1 + 2 * (n - 1) + 2 * (ten - 1),
+        n * ten - 1 + n - 1 + seq - 1 + 2 * (ten - 1),
         5,
         ident,
-        "outtake",
-    )
-
-
-def full_sum(partial_rows):
-    return lax.psum_scatter(
-        partial_rows, ("dp", "seq", "tensor"), scatter_dimension=0, tiled=True
-    ).astype(jnp.float32)
+    )
+
+
+def add_rows(target, sources):
+    step = 16
+
+    def body(at, carry):
+        rows = pl.ds(at * step, step)
+        total = target[rows].astype(jnp.float32)
+        for source in sources:
+            total += source[rows].astype(jnp.float32)
+        target[rows] = total.astype(target.dtype)
+        return carry
+
+    lax.fori_loop(0, target.shape[0] // step, body, 0)
+
+
+def full_sum_kernel(
+    sizes, parts, total, ssem, rsem, lsem, held, from_inner, front_one, back_one, front_two,
+    back_two, from_dp, result,
+):
+    dp, seq, ten = sizes
+    inner = parts.shape[2]
+    outer = seq // inner
+    z, s, t = lax.axis_index("dp"), lax.axis_index("seq"), lax.axis_index("tensor")
+    y, c = lax.div(s, inner), lax.rem(s, inner)
+    half = parts.shape[-1] // 2
+    front, back = pl.ds(0, half), pl.ds(half, half)
+    to_dp = [{"dp": shifted(z, o, dp)} for o in range(1, dp)]
+    ten_at = [shifted(t, o, ten) for o in range(ten)]
+    outer_at = [shifted(y, o, outer) for o in range(outer)]
+    inner_at = [shifted(c, o, inner) for o in range(inner)]
+    to_ten = [{"tensor": at} for at in ten_at]
+    to_outer = [{"seq": at * inner + c} for at in outer_at]
+    to_inner = [{"seq": y * inner + at} for at in inner_at]
+    greet(to_dp + to_ten[1:] + to_outer[1:] + to_inner[1:])
+    net = Net(ssem, rsem)
+    order = list(range(1, dp)) + [0]
+    goal = [shifted(z, k, dp) for k in range(dp)]
+    first, second, third, fourth, own = {}, {}, {}, {}, {}
+    for k in order:
+        own[k] = pltpu.make_async_copy(parts.at[goal[k], :, c], held.at[k], lsem.at[k])
+        own[k].start()
+        first[k] = [
+            net.send(parts.at[goal[k], :, inner_at[o]], from_inner.at[k, o - 1], to_inner[o])
+            for o in range(1, inner)
+        ]
+    for step in range(dp + 3):
+        if step < dp:
+            k = order[step]
+            own[k].wait()
+            for copy in first[k]:
+                copy.wait_recv()
+            for a in range(outer):
+                for b in range(ten):
+                    add_rows(
+                        held.at[k, a, b], [from_inner.at[k, o, a, b] for o in range(inner - 1)]
+                    )
+            second[k] = [
+                net.send(
+                    held.at[k, outer_at[o], :, :, front], front_one.at[k, o - 1], to_outer[o]
+                )
+                for o in range(1, outer)
+            ] + [
+                net.send(held.at[k, :, ten_at[o], :, back], back_one.at[k, o - 1], to_ten[o])
+                for o in range(1, ten)
+            ]
+        if 0 <= step - 1 < dp:
+            k = order[step - 1]
+            for copy in second[k]:
+                copy.wait_recv()
+            for b in range(ten):
+                add_rows(
+                    held.at[k, y, b, :, front], [front_one.at[k, o, b] for o in range(outer - 1)]
+                )
+            for a in range(outer):
+                add_rows(
+                    held.at[k, a, t, :, back], [back_one.at[k, o, a] for o in range(ten - 1)]
+                )
+            third[k] = [
+                net.send(held.at[k, y, ten_at[o], :, front], front_two.at[k, o - 1], to_ten[o])
+                for o in range(1, ten)
+            ] + [
+                net.send(held.at[k, outer_at[o], t, :, back], back_two.at[k, o - 1], to_outer[o])
+                for o in range(1, outer)
+            ]
+        if 0 <= step - 2 < dp:
+            k = order[step - 2]
+            for copy in third[k]:
+                copy.wait_recv()
+            add_rows(held.at[k, y, t, :, front], [front_two.at[k, o] for o in range(ten - 1)])
+            add_rows(held.at[k, y, t, :, back], [back_two.at[k, o] for o in range(outer - 1)])
+            if k:
+                fourth[k] = net.send(held.at[k, y, t], from_dp.at[k - 1], to_dp[k - 1])
+    result[...] = held[0, y, t].astype(jnp.float32)
+    for k in range(1, dp):
+        fourth[k].wait_recv()
+        add_rows(result, [from_dp.at[k - 1]])
+    out = pltpu.make_async_copy(result, total, lsem.at[dp])
+    out.start()
+    out.wait()
+    net.drain()
+
+
+def full_sum(sizes, partial_rows, ident):
+    dp, seq, ten = sizes
+    inner = 2 if seq % 2 == 0 else 1
+    outer = seq // inner
+    width = partial_rows.shape[1]
+    rows = partial_rows.shape[0] // (dp * seq * ten)
+    half, bf = width // 2, partial_rows.dtype
+    parts = partial_rows.reshape(dp, outer, inner, ten, rows, width)
+    some = lambda count: max(count, 1)
+    (total,) = call_kernel(
+        functools.partial(full_sum_kernel, sizes),
+        (parts,),
+        [jax.ShapeDtypeStruct((rows, width), jnp.float32)],
+        [False],
+        dp - 1 + dp * (2 * (ten - 1) + 2 * (outer - 1) + inner - 1),
+        dp + 1,
+        ident,
+        [
+            pltpu.VMEM((dp, outer, ten, rows, width), bf),
+            pltpu.VMEM((dp, some(inner - 1), outer, ten, rows, width), bf),
+            pltpu.VMEM((dp, some(outer - 1), ten, rows, half), bf),
+            pltpu.VMEM((dp, some(ten - 1), outer, rows, half), bf),
+            pltpu.VMEM((dp, some(ten - 1), rows, half), bf),
+            pltpu.VMEM((dp, some(outer - 1), rows, half), bf),
+            pltpu.VMEM((some(dp - 1), rows, width), bf),
+            pltpu.VMEM((rows, width), jnp.float32),
+        ],
+    )
+    return total
+
+
+def across_planes(dp, blocks):
+    z = lax.axis_index("dp")
+    leave = [lax.dynamic_index_in_dim(blocks, shifted(z, o, dp), 0) for o in range(1, dp)]
+    *leave, blocks = lax.optimization_barrier((*leave, blocks))
+    came = []
+    for o, block in enumerate(leave, 1):
+        came.append(lax.ppermute(block, "dp", [(i, (i + o) % dp) for i in range(dp)]))
+    *came, blocks = lax.optimization_barrier((*came, blocks))
+    for o, block in enumerate(came, 1):
+        blocks = lax.dynamic_update_slice_in_dim(blocks, block, shifted(z, dp - o, dp), 0)
+    return blocks
 
 
 def norm_forward(stream, gain):
@@ -386,7 +525,7 @@
     return jnp.einsum(spec, left, right, preferred_element_type=jnp.float32)
 
 
-def shards(
+def layer(
     sizes,
     tokens,
     positions,
@@ -408,7 +547,7 @@
     band = w_query.shape[1]
     rows = piece // ten
     length = piece * seq
-    s, t = lax.axis_index("seq"), lax.axis_index("tensor")
+    t = lax.axis_index("tensor")
 
     q_cols = w_query.shape[2] // seq
     kv_local = w_key.shape[2] // HD
@@ -438,8 +577,12 @@
         return jnp.pad(values, ((0, 7), (0, span - values.shape[1])))
 
     notes = jnp.concatenate([note(gain_attn), note(gain_ffn), note(positions)], axis=0)
-    all_cotangent = lax.all_gather(cotangent[0], ("dp", "seq"), axis=0, tiled=True)
-    all_a, all_f, pieces, all_notes = intake(sizes, pack_a, pack_f, tokens[0], notes, 0)
+    all_a, staged_f, pieces, all_notes = intake(
+        sizes, pack_a, pack_f.reshape(dp, seq, band, -1), tokens[0], notes, 0
+    )
+    all_f = across_planes(dp, staged_f.reshape(dp, seq * band, -1))
+    ready, _ = lax.optimization_barrier((cotangent[0], all_notes))
+    all_cotangent = lax.all_gather(ready, ("dp", "seq"), axis=0, tiled=True)
     gain_one = all_notes[:, 0, :band].reshape(1, width)
     gain_two = all_notes[:, 8, :band].reshape(1, width)
     z = lax.axis_index("dp")
@@ -485,11 +628,13 @@
     gate_grad = (hidden_grad * up * sigmoid_gate * (1.0 + gate * (1.0 - sigmoid_gate))).astype(bf)
     up_grad = (hidden_grad * gate * sigmoid_gate).astype(bf)
     gu_grad = jnp.concatenate([gate_grad, up_grad], axis=-1)
-    normed_two_grad = full_sum(dot_last(gu_grad, w_gu).astype(bf))
-    row_out = after_attn + full_sum(dot_last(hidden, w_d).astype(bf))
+    normed_two_grad = full_sum(sizes, dot_last(gu_grad, w_gu).astype(bf), 6)
+    down = dot_last(hidden, w_d).astype(bf)
+    down = lax.psum_scatter(down, ("dp", "seq", "tensor"), scatter_dimension=0, tiled=True)
     grad_f = jnp.concatenate(
         [dot_rows(normed_two, gu_grad), dot_rows(all_cotangent, hidden)], axis=-1
     ).astype(bf)
+    grad_f = across_planes(dp, grad_f.reshape(dp, seq * band, -1))
 
     row_cotangent = own_rows(cotangent[0]).astype(jnp.float32)
     part, gain_two_grad = norm_backward(after_attn, inverse_two, gain_two, normed_two_grad)
@@ -517,6 +662,8 @@
         [dot_rows(normed_one, qkv_grad), dot_rows(resid_low, flat_attended)], axis=-1
     ).astype(bf)
     normed_one_grad = plane_sum(sizes, dot_last(qkv_grad, w_qkv).astype(bf), 4)
+    down, normed_one_grad = lax.optimization_barrier((down, normed_one_grad))
+    row_out = after_attn + down.astype(jnp.float32)
     inverse_one = lax.rsqrt(jnp.mean(row_stream * row_stream, axis=-1, keepdims=True) + epsilon)
     part, gain_one_grad = norm_backward(row_stream, inverse_one, gain_one, normed_one_grad)
     row_grad = resid_grad + part
@@ -526,14 +673,14 @@
     got_a, got_f, got_gains, pair_grad, pair_out = outtake(
         sizes,
         grad_a.reshape(n, band, -1),
-        grad_f.reshape(n, band, -1),
+        grad_f.reshape(dp, seq, band, -1),
         gains,
         row_grad,
         row_out.astype(bf),
         5,
     )
     got_a = jnp.sum(got_a.reshape(dp, seq, band, -1).astype(jnp.float32), axis=0)
-    got_f = got_f.astype(jnp.float32)
+    got_f = got_f.reshape(n, band, -1).astype(jnp.float32)
     got_gains = jnp.sum(got_gains, axis=(0, 1, 2))
 
     def spread(block):
@@ -565,7 +712,7 @@
     out_specs = (rows, rows, gain, gain) + (weight,) * 7
     sizes = (mesh.shape["dp"], mesh.shape["seq"], mesh.shape["tensor"])
     return jax.shard_map(
-        functools.partial(shards, sizes),
+        functools.partial(layer, sizes),
         mesh=mesh,
         in_specs=in_specs,
         out_specs=out_specs,

time: 970 us -> 777 us (0.80)
  waiting for transfers between devices: 336 us -> 62.5 us
  Pallas kernels: 441 us -> 498 us
  local copies, waits for them, and re-layouts: 66.2 us -> 81.4 us
    reduce_scatter x2 -> x1, waiting for transfers between devices: 335 us -> 0.01 us  [layer(): lax.psum_scatter(down, ('dp', 'seq', 'tensor'), scatter_dimension=0, tile...]
    ppermute x0 -> x6, waiting for transfers between devices: none -> 62.5 us  [across_planes(): lax.ppermute(block, 'dp', [(i, (i + o) % dp) for i in range(dp)])]
    pallas_call x6 -> x7, Pallas kernels: 441 us -> 498 us  [call_kernel(): pl.pallas_call(body, out_shape=outputs, in_specs=spaces, out_specs=[pl.Bl...]
    dynamic_update_slice x0 -> x7, local copies, waits for them, and re-layouts: none -> 13.9 us  [across_planes(): lax.dynamic_update_slice_in_dim(blocks, block, shifted(z, dp - o, dp), 0)]
    unnamed x114 -> x107, local copies, waits for them, and re-layouts: 23.7 us -> 19.5 us
  transfers between devices with their start and end apart: 3 -> 8, of which waited for: 2 -> 3; matrix products, arithmetic and copies ran while one was open for 9% -> 15% of each run, Pallas kernels for 26% -> 43%
where the time goes in v2:
time: 777 us; the launch traced here: 769 us
  Pallas kernels  498 us (64%)
  local copies, waits for them, and re-layouts  81.4 us (10%)
  matrix products  77 us (10%)
  waiting for transfers between devices  62.5 us (8%)
  other arithmetic  28.1 us (4%)
  between operations  15.2 us (2%)
    pallas_call x7, Pallas kernels, call_kernel(): pl.pallas_call(body, out_shape=outputs, in_specs=spaces, out_specs=[pl.Bl...  498 us
    ppermute x6, waiting for transfers between devices, across_planes(): lax.ppermute(block, 'dp', [(i, (i + o) % dp) for i in range(dp)])  62.5 us
    dot_general x4, matrix products, dot_last(): lax.dot_general(left, right, (((1,), (1,)), ((), ())), preferred_element_...  24.7 us
    dot_general x4, matrix products, dot(): return jnp.dot(left, right, preferred_element_type=jnp.float32)  24.2 us
    unnamed x107, local copies, waits for them, and re-layouts  19.5 us
    dot_general x3, local copies, waits for them, and re-layouts, dot_rows(): lax.dot_general(left, right, (((0,), (0,)), ((), ())), preferred_element_...  18.8 us
    transpose x10, local copies, waits for them, and re-layouts, spread(): return jnp.moveaxis(block, 0, 1).reshape(1, band, -1)  17 us
    dot_general x4, matrix products, dot_rows(): lax.dot_general(left, right, (((0,), (0,)), ((), ())), preferred_element_...  16.5 us
  transfers between devices with their start and end apart: 8, of which 3 were waited for; matrix products, arithmetic and copies ran while one was open for 15% of the time, Pallas kernels for 43%

profile of v2, /device:TPU:9, one launch (start us, length us, event | category | flops | bytes accessed | tf_op | source)
XLA Modules:
  0.0 769.4 jit_solution(3124942097930442481)
XLA Ops:
  18.4 94.5 %shard_map.203 = (bf16[16,128,640]{2,1,0:T(8,128)(2,1)}, bf16[4,4,128,768]{3,2,1,0:T(8,128)(2,1)}, bf16[4,128,2048]{2,1,0:T(8,128)(2,1)}, f32[16,24,128]{2,1,0:T(8,128)}) custom-call(bf16[4,128,640]{2,1,0:T(8,128)(2,1)} %pad_maximum_fusion.6.pack_a, bf16[4,4,128,768]{3,2,1,0:T(8,128)(2,1)} %bitcast.245, bf16[128,2048]{1,0:T(8,128)(2,1)} %bitcast.264, ...), custom_call_target="tpu_custom_call" | custom-call | bytes 173506560 | tf_op jit(solution)/shard_map/pallas_call | solution.py:57
  113.0 3.2 constant_dynamic-slice_fusion
  116.5 3.0 collective-permute-start.1
  128.8 3.3 convolution_convert_fusion.2
  132.1 26.6 %shard_map.204 = bf16[7,64,2048]{2,1,0:T(8,128)(2,1)} custom-call(bf16[4,2,64,2048]{3,2,1,0:T(8,128)(2,1)} %bitcast.246), custom_call_target="tpu_custom_call" | custom-call | bytes 83886080 | tf_op jit(solution)/shard_map/pallas_call | solution.py:57
  163.1 117.8 %shard_map.205 = bf16[4,2,2,2,64,2048]{5,4,3,2,1,0:T(8,128)(2,1)} custom-call(bf16[64,2048]{1,0:T(8,128)(2,1)} %multiply_convert_fusion.3.rows), custom_call_target="tpu_custom_call" | custom-call | bytes 10485760 | tf_op jit(solution)/shard_map/pallas_call | solution.py:57
  287.2 10.9 %fusion.23 = f32[2048,512]{0,1:T(8,128)} fusion(bf16[2048,2048]{1,0:T(8,128)(2,1)} %bitcast.242, bf16[2048,768]{1,0:T(8,128)(2,1)} %bitcast.260), kind=kOutput, calls=%fused_computation.52 | convolution fusion | flops 4294967296 | bytes 14680064 | tf_op jit(solution)/shard_map/dot_general | solution.py:509
  298.2 9.5 %multiply_convert_fusion.2 = (bf16[2048,256]{0,1:T(8,128)(2,1)}, bf16[2048,256]{0,1:T(8,128)(2,1)}, bf16[2048,256]{0,1:T(8,128)(2,1)S(1)}) fusion(f32[2048,512]{0,1:T(8,128)} %fusion.23, bf16[2048,2048]{1,0:T(8,128)(2,1)} %all-gather.2.cloned.1.call-done, bf16[2048,768]{1,0:T(8,128)(2,1)} %bitcast.261), kind=kOutput, calls=%fused_computation.47 | convolution fusion | flops 2155872256 | bytes 16777216 | tf_op jit(solution)/shard_map/dot_general | solution.py:509
  307.6 7.3 convolution_convert_fusion
  316.5 2.5 copy.114
  319.0 12.4 %copy.124 = bf16[2048,2048]{1,0:T(8,128)(2,1)} copy(bf16[2048,2048]{0,1:T(8,128)(2,1)} %bitcast.243) | data formatting | bytes 16777216 | tf_op jit(solution)/shard_map/dot_general | solution.py:519
  331.9 6.0 convolution_convert_fusion.4
  338.5 10.1 %convolution_convert_fusion.1 = bf16[2048,2048]{1,0:T(8,128)(2,1)} fusion(bf16[2048,768]{1,0:T(8,128)(2,1)} %bitcast.263, bf16[2048,256]{0,1:T(8,128)(2,1)} %get-tuple-element.110, bf16[2048,256]{0,1:T(8,128)(2,1)} %get-tuple-element.109), kind=kOutput, calls=%fused_computation.1 | convolution fusion | flops 4303355904 | bytes 12582912 | tf_op jit(solution)/shard_map/dot_general | solution.py:513
  348.6 86.9 %shard_map.206 = f32[64,2048]{1,0:T(8,128)} custom-call(bf16[4,2,2,2,64,2048]{5,4,3,2,1,0:T(8,128)(2,1)} %bitcast.249), custom_call_target="tpu_custom_call" | custom-call | bytes 335544320 | tf_op jit(solution)/shard_map/pallas_call | solution.py:57
  439.8 51.9 %shard_map.207 = bf16[4,2,64,2048]{3,2,1,0:T(8,128)(2,1)} custom-call(bf16[64,2048]{1,0:T(8,128)(2,1)} %fusion.97.rows), custom_call_target="tpu_custom_call" | custom-call | bytes 10485760 | tf_op jit(solution)/shard_map/pallas_call | solution.py:57
  491.7 2.8 convolution_convert_fusion.7
  495.2 2.6 fusion.2
  499.9 2.5 fusion.37
  503.5 3.6 fusion.43
  507.3 4.0 convolution_convert_fusion.3
  511.3 49.6 %shard_map.208 = bf16[7,64,2048]{2,1,0:T(8,128)(2,1)} custom-call(bf16[4,2,64,2048]{3,2,1,0:T(8,128)(2,1)} %bitcast.265), custom_call_target="tpu_custom_call" | custom-call | bytes 83886080 | tf_op jit(solution)/shard_map/pallas_call | solution.py:57
  561.0 3.9 copy.122
  564.9 8.5 %fusion.19 = bf16[4,512,512]{1,2,0:T(8,128)(2,1)S(1)} fusion(bf16[4,512,2048]{2,1,0:T(8,128)(2,1)} %bitcast.248, bf16[2048,256]{0,1:T(8,128)(2,1)} %get-tuple-element.110, bf16[2048,256]{0,1:T(8,128)(2,1)} %get-tuple-element.109), kind=kOutput, calls=%fused_computation.50 | convolution fusion | flops 4300210176 | bytes 12582912 | tf_op jit(solution)/shard_map/dot_general | solution.py:519
  584.8 11.3 %collective-permute-done.3 = bf16[1,512,768]{1,2,0:T(8,128)(2,1)S(1)} collective-permute-done((bf16[1,512,768]{1,2,0:T(8,128)(2,1)S(1)}, bf16[1,512,768]{1,2,0:T(8,128)(2,1)S(1)}, u32[]{:S(2)}, u32[]{:S(2)}) %collective-permute-start.3) | collective-permute-done | bytes 786464 | tf_op jit(solution)/shard_map/ppermute | solution.py:466
  596.1 49.1 %collective-permute-done.4 = bf16[1,512,768]{1,2,0:T(8,128)(2,1)S(1)} collective-permute-done((bf16[1,512,768]{1,2,0:T(8,128)(2,1)S(1)}, bf16[1,512,768]{1,2,0:T(8,128)(2,1)S(1)}, u32[]{:S(2)}, u32[]{:S(2)}) %collective-permute-start.4) | collective-permute-done | bytes 786464 | tf_op jit(solution)/shard_map/ppermute | solution.py:466
  650.1 4.7 copy.126
  658.0 70.6 %shard_map.209 = (bf16[16,128,640]{2,1,0:T(8,128)(2,1)}, bf16[4,4,128,768]{3,2,1,0:T(8,128)(2,1)}, f32[4,4,2,8,128]{4,3,2,1,0:T(8,128)}, f32[2,64,2048]{2,1,0:T(8,128)}, bf16[2,64,2048]{2,1,0:T(8,128)(2,1)}) custom-call(bf16[16,128,640]{2,1,0:T(8,128)(2,1)} %pad_maximum_fusion.2.grad_a, bf16[4,4,128,768]{3,2,1,0:T(8,128)(2,1)} %bitcast.244, ...), custom_call_target="tpu_custom_call" | custom-call | bytes 264765440 | tf_op jit(solution)/shard_map/pallas_call | solution.py:57
  728.6 2.3 convert_reduce_fusion
  733.3 2.3 copy.130
  745.4 2.7 slice_bitcast_fusion
  750.8 2.8 copy.132
  755.2 2.8 copy.131
  (196 shorter events, 82.2 us)
Async XLA Ops:
  7.2 5.7 copy-start.17
  7.2 291.0 %all-gather.2.cloned.1.call-start = ((), (), s32[]{:S(2)}) async-start(), calls=%async_computation.1 | async-start | bytes 8912896 | tf_op jit(solution)/shard_map/all_gather | solution.py:585
  112.9 6.8 copy-start.1
  112.9 542.0 %reduce-scatter.2.cloned.1.call-start = ((), (), s32[]{:S(2)}) async-start(), calls=%async_computation.2 | async-start | bytes 8650752 | tf_op jit(solution)/shard_map/reduce_scatter | solution.py:633
  116.2 164.7 %collective-permute-start = (bf16[1,512,768]{2,1,0:T(8,128)(2,1)}, bf16[1,512,768]{2,1,0:T(8,128)(2,1)}, u32[]{:S(2)}, u32[]{:S(2)}) collective-permute-start(bf16[1,512,768]{2,1,0:T(8,128)(2,1)} %get-tuple-element.44), channel_id=1, source_target_pairs={{0,8},{8,16},{16,24},{24,0},{1,9},{9,17},{17,25},{25,1},{2,10},{10... | collective-permute-start | bytes 2359304 | tf_op jit(solution)/shard_map/ppermute | solution.py:466
  116.5 164.4 %collective-permute-start.1 = (bf16[1,512,768]{2,1,0:T(8,128)(2,1)}, bf16[1,512,768]{2,1,0:T(8,128)(2,1)}, u32[]{:S(2)}, u32[]{:S(2)}) collective-permute-start(bf16[1,512,768]{2,1,0:T(8,128)(2,1)} %get-tuple-element.45), channel_id=1, source_target_pairs={{0,16},{8,24},{16,0},{24,8},{1,17},{9,25},{17,1},{25,9},{2,18},{10... | collective-permute-start | bytes 2359304 | tf_op jit(solution)/shard_map/ppermute | solution.py:466
  119.5 161.4 %collective-permute-start.2 = (bf16[1,512,768]{2,1,0:T(8,128)(2,1)}, bf16[1,512,768]{2,1,0:T(8,128)(2,1)}, u32[]{:S(2)}, u32[]{:S(2)}) collective-permute-start(bf16[1,512,768]{2,1,0:T(8,128)(2,1)} %get-tuple-element.46), channel_id=1, source_target_pairs={{0,24},{8,0},{16,8},{24,16},{1,25},{9,1},{17,9},{25,17},{2,26},{10... | collective-permute-start | bytes 2359304 | tf_op jit(solution)/shard_map/ppermute | solution.py:466
  119.7 3.7 copy-start.24
  132.1 28.5 %copy-start.9 = (bf16[1,128,2048]{2,1,0:T(8,128)(2,1)S(1)}, bf16[1,128,2048]{2,1,0:T(8,128)(2,1)}, u32[]{:S(2)}) copy-start(bf16[1,128,2048]{2,1,0:T(8,128)(2,1)} %param.12) | copy-start | bytes 1572868
  162.3 118.6 %copy-start.33 = (f32[64]{0:T(128)}, f32[64]{0:T(128)S(1)}, u32[]{:S(2)}) copy-start(f32[64]{0:T(128)S(1)} %add_rsqrt_fusion.1) | copy-start | bytes 772
  307.6 7.3 copy-start.13
  319.0 12.4 %copy-start.44 = (f32[64]{0:T(128)S(1)}, f32[64]{0:T(128)}, u32[]{:S(2)}) copy-start(f32[64]{0:T(128)} %get-tuple-element.128) | copy-start | bytes 772
  319.0 12.9 %copy-start.14 = (bf16[2048,256]{0,1:T(8,128)(2,1)S(1)}, bf16[2048,256]{0,1:T(8,128)(2,1)}, u32[]{:S(2)}) copy-start(bf16[2048,256]{0,1:T(8,128)(2,1)} %copy-done.13) | copy-start | bytes 3145732
  348.6 86.9 %copy-start.34 = (f32[64]{0:T(128)S(1)}, f32[64]{0:T(128)}, u32[]{:S(2)}) copy-start(f32[64]{0:T(128)} %copy-done.33) | copy-start | bytes 772
  348.6 89.2 %copy-start.11 = (bf16[1,128,2048]{2,1,0:T(8,128)(2,1)S(1)}, bf16[1,128,2048]{2,1,0:T(8,128)(2,1)}, u32[]{:S(2)}) copy-start(bf16[1,128,2048]{2,1,0:T(8,128)(2,1)} %param.23) | copy-start | bytes 1572868
  439.8 55.4 %copy-start.16 = (pred[512,512]{0,1:T(8,128)(4,1)S(1)}, pred[512,512]{0,1:T(8,128)(4,1)}, u32[]{:S(2)}) copy-start(pred[512,512]{0,1:T(8,128)(4,1)} %copy-done.15) | copy-start | bytes 786436
  491.6 3.5 copy-start.8
  491.6 3.5 copy-start.37
  491.6 3.5 copy-start.39
  495.2 4.0 copy-start.27
  495.2 4.0 copy-start.29
  573.6 5.8 copy-start.4
  575.5 4.7 copy-start.12
  575.5 20.6 %collective-permute-start.3 = (bf16[1,512,768]{1,2,0:T(8,128)(2,1)S(1)}, bf16[1,512,768]{1,2,0:T(8,128)(2,1)S(1)}, u32[]{:S(2)}, u32[]{:S(2)}) collective-permute-start(bf16[1,512,768]{1,2,0:T(8,128)(2,1)S(1)} %get-tuple-element.52), channel_id=1, source_target_pairs={{0,8},{8,16},{16,24},{24,0},{1,9},{9,17},{17,25},{25,1},{2,10},{10... | collective-permute-start | bytes 2359304 | tf_op jit(solution)/shard_map/ppermute | solution.py:466
  576.3 68.8 %collective-permute-start.4 = (bf16[1,512,768]{1,2,0:T(8,128)(2,1)S(1)}, bf16[1,512,768]{1,2,0:T(8,128)(2,1)S(1)}, u32[]{:S(2)}, u32[]{:S(2)}) collective-permute-start(bf16[1,512,768]{1,2,0:T(8,128)(2,1)S(1)} %get-tuple-element.53), channel_id=1, source_target_pairs={{0,16},{8,24},{16,0},{24,8},{1,17},{9,25},{17,1},{25,9},{2,18},{10... | collective-permute-start | bytes 2359304 | tf_op jit(solution)/shard_map/ppermute | solution.py:466
  578.6 68.7 %collective-permute-start.5 = (bf16[1,512,768]{1,2,0:T(8,128)(2,1)S(1)}, bf16[1,512,768]{1,2,0:T(8,128)(2,1)S(1)}, u32[]{:S(2)}, u32[]{:S(2)}) collective-permute-start(bf16[1,512,768]{1,2,0:T(8,128)(2,1)S(1)} %get-tuple-element.54), channel_id=1, source_target_pairs={{0,24},{8,0},{16,8},{24,16},{1,25},{9,1},{17,9},{25,17},{2,26},{10... | collective-permute-start | bytes 2359304 | tf_op jit(solution)/shard_map/ppermute | solution.py:466
  650.1 4.8 copy-start.43
  650.1 5.1 copy-start
  650.1 5.1 copy-start.35
  650.1 5.1 copy-start.42
  728.6 4.2 copy-start.30
  732.8 11.7 %copy-start.10 = (bf16[4,4,128,768]{3,2,1,0:T(8,128)(2,1)S(1)}, bf16[4,4,128,768]{3,2,1,0:T(8,128)(2,1)}, u32[]{:S(2)}) copy-start(bf16[4,4,128,768]{3,2,1,0:T(8,128)(2,1)} %get-tuple-element.66) | copy-start | bytes 9437188
  (23 other events, 43.2 us)
Sparse Core Ops, SparseCore 0:
  113.1 134.6 all-gather.1
  315.1 270.0 reduce-scatter.1
